TPU v7x, 32 devices: a whole 2x2x4 slice. The times are simulated.
32 devices in a mesh: gx: 4 (over y, core), gy: 2 (over x), gz: 4 (over z).
Axes of the slice: x: 2, y: 2, z: 4, core: 2. Of those that a mesh axis runs over, the one named last changes fastest.
Arguments:
- source: float32 [256, 128, 128], P('gx', 'gy', 'gz'), may hold values from -6 to 6
- green: float32 [512, 256, 256], P(None, ('gx', 'gz'), 'gy'), may hold values from 0.05 to 2, as said below
Outputs:
- potential: float32 [256, 128, 128], P('gx', 'gy', 'gz')
Inputs may be any that keep to these rules, and one draw needn't show every extreme that they name: `green`: greenfull is even: greenfull[k] equals greenfull at (-k1 mod 512, -k2 mod 256, -k3 mod 256).
All inputs are finite; a program needn't handle non-finite values.
Results may differ from a plain program's by a relative error of at most 0.00007.
Values sent between devices are 32-bit elements; how exact they have to be, the bound alone decides.
No kernel may reach another device: no remote copies, remote signals or barrier semaphores. Data moves between devices by JAX's collectives and lax.ppermute only.
A program may use at most 128 MiB of HBM per device.

v0:
```python
import math

import jax
import jax.numpy as jnp
import numpy as np
from jax import lax
from jax.experimental import pallas as pl
from jax.experimental.pallas import tpu as pltpu
from jax.sharding import PartitionSpec as P

LANES = 128
SUBS = 8


def pair_frequency(length):
    position = np.arange(length)
    unit = position // 2
    member = position % 2
    return np.where(unit == 0, member * (length // 2), np.where(member == 0, unit, length - unit))


def trig(rows, cols, length):
    angles = (rows[:, None] * cols[None, :] % length) * (2.0 * math.pi / length)
    return np.cos(angles), np.sin(angles)


def split_table(table):
    table = np.asarray(table, np.float32)
    high = table.astype(jnp.bfloat16)
    low = (table - high.astype(np.float32)).astype(jnp.bfloat16)
    return jnp.asarray(high), jnp.asarray(low)


def halves(value):
    high = value.astype(jnp.bfloat16)
    low = (value - high.astype(jnp.float32)).astype(jnp.bfloat16)
    return high, low


def mm(a, b):
    dot = lambda p, q: jnp.dot(p, q, preferred_element_type=jnp.float32)
    return dot(a[0], b[0]) + (dot(a[0], b[1]) + dot(a[1], b[0]))


def call(body, out_shape, operands, scratch=(), specs=None):
    vmem = pl.BlockSpec(memory_space=pltpu.VMEM)
    return pl.pallas_call(
        body,
        out_shape=out_shape,
        in_specs=specs or [vmem] * len(operands),
        out_specs=jax.tree.map(lambda _: vmem, out_shape),
        scratch_shapes=list(scratch),
        compiler_params=pltpu.CompilerParams(vmem_limit_bytes=56 * 2**20),
    )(*operands)


def block_transpose(pieces, brick):
    count = len(pieces)
    lane = lax.broadcasted_iota(jnp.int32, pieces[0].shape, 1) // brick
    pieces = list(pieces)
    step = 1
    while step < count:
        odd = (lane // step) % 2 == 1
        for at in range(count):
            if (at // step) % 2 == 0:
                low, high = pieces[at], pieces[at + step]
                pieces[at] = jnp.where(odd, pltpu.roll(high, step * brick, 1), low)
                pieces[at + step] = jnp.where(
                    odd, high, pltpu.roll(low, LANES - step * brick, 1)
                )
        step *= 2
    return pieces


def per_device(source, green):
    size_gx = lax.axis_size("gx")
    size_gy = lax.axis_size("gy")
    size_gz = lax.axis_size("gz")
    brick_x, brick_y, brick_z = source.shape
    grid_x, grid_y, grid_z = brick_x * size_gx, brick_y * size_gy, brick_z * size_gz
    long_x, long_y, long_z = 2 * grid_x, 2 * grid_y, 2 * grid_z
    group = size_gx * size_gz
    part_x = brick_x // size_gy
    per_tile = LANES // brick_z
    tiles_x = part_x // per_tile
    tiles_z = grid_z // LANES
    rows_c = tiles_x * SUBS
    count_k = long_z // size_gy
    units = grid_y
    f32 = jnp.float32
    h = lax.axis_index("gy")
    first = (lax.axis_index("gx") * size_gz + lax.axis_index("gz") == 0).astype(jnp.int32)
    where = jnp.stack([h.astype(jnp.int32), first])
    smem = pl.BlockSpec(memory_space=pltpu.SMEM)
    vmem = pl.BlockSpec(memory_space=pltpu.VMEM)

    def shift(value, step):
        perm = [(i, (i + step) % size_gy) for i in range(size_gy)]
        return lax.ppermute(value, "gy", perm)

    def pack_body(where_ref, src_ref, *outs):
        for step in range(size_gy):
            base = (where_ref[0] + step) % size_gy * part_x
            for c in range(tiles_x):
                outs[step][:, c * LANES : (c + 1) * LANES] = jnp.concatenate(
                    [src_ref[base + c * per_tile + p] for p in range(per_tile)], axis=1
                )

    packed = call(
        pack_body,
        [jax.ShapeDtypeStruct((brick_y, tiles_x * LANES), f32)] * size_gy,
        (where, source),
        specs=[smem, vmem],
    )
    lines = [packed[0]] + [shift(packed[s], s) for s in range(1, size_gy)]

    sign_y = 1.0 - 2.0 * (np.arange(grid_y) % 2)
    cos_y, sin_y = trig(np.arange(units), np.arange(grid_y), long_y)
    im_y = -sin_y
    im_y[0] = sign_y
    fwd_y = np.concatenate([cos_y, im_y], 0)
    fwd_y = fwd_y.reshape(2 * units, size_gy, brick_y).transpose(1, 0, 2)
    fwd_y = split_table(fwd_y)

    def y_body(where_ref, high_ref, low_ref, *refs):
        ins, outs = refs[:size_gy], refs[size_gy:]
        total = None
        for s in range(size_gy):
            block = (where_ref[0] + size_gy - s) % size_gy
            term = mm((high_ref[block], low_ref[block]), halves(ins[s][...]))
            total = term if total is None else total + term
        for part in range(2):
            for c in range(tiles_x):
                piece = total[part * units : (part + 1) * units, c * LANES : (c + 1) * LANES]
                outs[part][:, c * SUBS : (c + 1) * SUBS, :] = piece.reshape(group, SUBS, LANES)

    plane = jax.ShapeDtypeStruct((group, rows_c, LANES), f32)
    spectra = call(
        y_body, [plane] * 2, (where, *fwd_y, *lines), specs=[smem] + [vmem] * (2 + size_gy)
    )

    def exchange(value):
        return lax.all_to_all(value, ("gx", "gz"), 0, 0, tiled=True)

    own = [exchange(v) for v in spectra]
    gathered = list(own)
    for s in range(1, size_gy):
        gathered += [shift(v, s) for v in own]

    freq_z = pair_frequency(long_z).reshape(size_gy, count_k)
    fwd_z, inv_z = [], []
    for block in range(size_gy):
        c, s = trig(np.arange(grid_z), freq_z[block], long_z)
        fwd_z.append(np.block([[c, -s], [s, c]]))
        inv_z.append(np.block([[c.T, s.T], [-s.T, c.T]]) / long_z)
    fwd_z = split_table(np.stack(fwd_z))
    inv_z = split_table(np.stack(inv_z))
    ih, ig, ip, ic = np.meshgrid(
        np.arange(size_gy), np.arange(size_gx), np.arange(per_tile), np.arange(tiles_x),
        indexing="ij",
    )
    order_x = (ig * brick_x + ih * part_x + ic * per_tile + ip).reshape(-1)
    cos_x, sin_x = trig(np.arange(grid_x), order_x, long_x)
    sin_x[0] = 1.0 - 2.0 * (order_x % 2)
    weight = np.where(np.arange(grid_x) == 0, 0.5, 1.0)[:, None] / long_x
    fwd_x = split_table(np.concatenate([cos_x, sin_x], 0))
    inv_x = split_table(np.concatenate([cos_x * weight, sin_x * weight], 0).T)
    own_rows = green.shape[1]
    green_rows = green.reshape(long_x * own_rows, count_k)
    block_rows = per_tile * rows_c

    def middle_body(where_ref, green_ref, edge_ref, fzh, fzl, izh, izl, fxh, fxl, ixh, ixl, *refs):
        ins = refs[: 2 * size_gy]
        outs = refs[2 * size_gy : 4 * size_gy]
        field = refs[4 * size_gy]
        here = where_ref[0]
        is_first = where_ref[1] == 1
        table_z = (fzh[here], fzl[here])
        back_z = (izh[here], izl[here])
        for s in range(size_gy):
            side = (here + size_gy - s) % size_gy
            for g in range(size_gx):
                cols = []
                for part in range(2):
                    ref = ins[2 * s + part]
                    for t in range(tiles_z):
                        at = g * size_gz + t * per_tile
                        cols.append(
                            jnp.concatenate(
                                block_transpose([ref[at + q] for q in range(per_tile)], brick_z), 0
                            )
                        )
                rows = jnp.concatenate(cols, 1)
                out = mm(halves(rows), table_z)
                offset = pl.multiple_of((side * size_gx + g) * block_rows, block_rows)
                field[pl.ds(offset, block_rows), :] = out[:, :count_k]
                field[pl.ds(size_rows + offset, block_rows), :] = out[:, count_k:]

        def mirror(value):
            lane = lax.broadcasted_iota(jnp.int32, value.shape, 1)
            swapped = jnp.where(
                lane % 2 == 0, pltpu.roll(value, count_k - 1, 1), pltpu.roll(value, 1, 1)
            )
            keep = jnp.logical_and(here == 0, lane < 2)
            return jnp.where(keep, value, swapped)

        def filtered(re, im, row_p, row_m):
            both = mm((fxh[...], fxl[...]), halves(jnp.concatenate([re, im], 1)))
            cr, ci = both[:grid_x, :count_k], both[:grid_x, count_k:]
            sr, si = both[grid_x:, :count_k], both[grid_x:, count_k:]
            gp = green_ref[pl.ds(row_p, grid_x, stride=own_rows), :]
            gm = mirror(green_ref[pl.ds(row_m, grid_x, stride=own_rows), :])
            ga, gb = gp + gm, gp - gm
            edge = edge_ref[pl.ds(row_p, 1), :] + mirror(edge_ref[pl.ds(row_m, 1), :])
            top = lax.broadcasted_iota(jnp.int32, ga.shape, 0) == 0
            gb = jnp.where(top, 0.0, gb)
            ge = jnp.where(top, edge, ga)
            even = jnp.concatenate([ga * cr + gb * si, ga * ci - gb * sr], 1)
            odd = jnp.concatenate([ge * sr - gb * ci, gb * cr + ge * si], 1)
            return mm((ixh[...], ixl[...]), halves(jnp.concatenate([even, odd], 0)))

        for u in range(SUBS):
            at_re = pl.ds(u, grid_x, stride=SUBS)
            at_im = pl.ds(size_rows + u, grid_x, stride=SUBS)
            if u == 0:

                @pl.when(is_first)
                def _():
                    re, im = field[at_re, :], field[at_im, :]
                    are = 0.5 * (re + mirror(re))
                    aim = 0.5 * (im - mirror(im))
                    out = filtered(are, aim, 0, 0) + filtered(re - are, im - aim, 1, 1)
                    field[at_re, :] = out[:, :count_k]
                    field[at_im, :] = out[:, count_k:]

                @pl.when(jnp.logical_not(is_first))
                def _():
                    out = filtered(field[at_re, :], field[at_im, :], 0, 1)
                    field[at_re, :] = out[:, :count_k]
                    field[at_im, :] = out[:, count_k:]
            else:
                out = filtered(field[at_re, :], field[at_im, :], 2 * u, 2 * u + 1)
                field[at_re, :] = out[:, :count_k]
                field[at_im, :] = out[:, count_k:]

        for s in range(size_gy):
            side = (here + size_gy - s) % size_gy
            for g in range(size_gx):
                offset = pl.multiple_of((side * size_gx + g) * block_rows, block_rows)
                rows = jnp.concatenate(
                    [
                        field[pl.ds(offset, block_rows), :],
                        field[pl.ds(size_rows + offset, block_rows), :],
                    ],
                    1,
                )
                out = mm(halves(rows), back_z)
                for part in range(2):
                    for t in range(tiles_z):
                        lo = (part * tiles_z + t) * LANES
                        col = out[:, lo : lo + LANES]
                        pieces = block_transpose(
                            [col[p * rows_c : (p + 1) * rows_c] for p in range(per_tile)], brick_z
                        )
                        for q in range(per_tile):
                            outs[2 * s + part][g * size_gz + t * per_tile + q] = pieces[q]

    size_rows = grid_x * SUBS
    operands = (where, green_rows, green_rows, *fwd_z, *inv_z, *fwd_x, *inv_x, *gathered)
    whole = lambda value: pl.BlockSpec(value.shape, lambda i: (0,) * value.ndim)
    returned = pl.pallas_call(
        middle_body,
        grid=(1,),
        out_shape=[plane] * (2 * size_gy),
        in_specs=[
            smem,
            pl.BlockSpec((grid_x * own_rows, count_k), lambda i: (0, 0)),
            pl.BlockSpec((own_rows, count_k), lambda i: (grid_x, 0)),
        ]
        + [whole(v) for v in operands[3:]],
        out_specs=[whole(plane)] * (2 * size_gy),
        scratch_shapes=[pltpu.VMEM((2 * size_rows, count_k), f32)],
        compiler_params=pltpu.CompilerParams(vmem_limit_bytes=56 * 2**20),
    )(*operands)
    summed = list(returned[:2])
    for s in range(1, size_gy):
        for part in range(2):
            summed[part] = summed[part] + shift(returned[2 * s + part], size_gy - s)
    last = [exchange(v) for v in summed]

    cos_b, sin_b = trig(np.arange(grid_y), np.arange(units), long_y)
    inv_re = 2.0 * cos_b
    inv_re[:, 0] = 1.0
    inv_im = -2.0 * sin_b
    inv_im[:, 0] = sign_y
    inv_y = np.concatenate([inv_re, inv_im], 1) / long_y
    inv_y = split_table(inv_y.reshape(size_gy, brick_y, 2 * units))

    def back_body(where_ref, high_ref, low_ref, re_ref, im_ref, *outs):
        rows = jnp.concatenate(
            [
                jnp.concatenate(
                    [
                        ref[:, c * SUBS : (c + 1) * SUBS, :].reshape(units, LANES)
                        for c in range(tiles_x)
                    ],
                    1,
                )
                for ref in (re_ref, im_ref)
            ],
            0,
        )
        rows = halves(rows)
        for s in range(size_gy):
            block = (where_ref[0] + s) % size_gy
            outs[s][...] = mm((high_ref[block], low_ref[block]), rows)

    lines = call(
        back_body,
        [jax.ShapeDtypeStruct((brick_y, tiles_x * LANES), f32)] * size_gy,
        (where, *inv_y, *last),
        specs=[smem] + [vmem] * 4,
    )
    lines = [lines[0]] + [shift(lines[s], s) for s in range(1, size_gy)]

    def unpack_body(where_ref, *refs):
        ins, out = refs[:size_gy], refs[size_gy]
        for s in range(size_gy):
            base = (where_ref[0] + size_gy - s) % size_gy * part_x
            for x in range(part_x):
                out[base + x] = ins[s][:, x * brick_z : (x + 1) * brick_z]

    return call(
        unpack_body,
        jax.ShapeDtypeStruct(source.shape, f32),
        (where, *lines),
        specs=[smem] + [vmem] * size_gy,
    )


def solution(mesh):
    return jax.shard_map(
        per_device,
        mesh=mesh,
        in_specs=(P("gx", "gy", "gz"), P(None, ("gx", "gz"), "gy")),
        out_specs=P("gx", "gy", "gz"),
        check_vma=False,
    )
```

profile of v0, /device:TPU:0, one launch (start us, length us, event | category | flops | bytes accessed | tf_op | source)
XLA Modules:
  0.0 159.2 jit_solution(704411334857915026)
XLA Ops:
  0.0 3.2 %copy.15.src_ref = f32[64,64,32]{2,1,0:T(8,128)} copy(f32[64,64,32]{1,2,0:T(8,128)} %param.14) | data formatting | bytes 1048576 | tf_op args[0]
  3.2 0.6 pad_add_fusion.where_ref
  3.8 2.8 %shard_map.136 = (f32[64,1024]{1,0:T(8,128)}, f32[64,1024]{1,0:T(8,128)}) custom-call(s32[2]{0:T(128)} %pad_add_fusion.where_ref, f32[64,64,32]{2,1,0:T(8,128)} %copy.15.src_ref), custom_call_target="tpu_custom_call" | custom-call | tf_op jit(solution)/shard_map/pallas_call | solution.py:47
  6.6 3.0 %collective-permute-start = (f32[64,1024]{1,0:T(8,128)}, f32[64,1024]{1,0:T(8,128)S(1)}, u32[]{:S(2)}, u32[]{:S(2)}) collective-permute-start(f32[64,1024]{1,0:T(8,128)} %get-tuple-element.16), channel_id=1, source_target_pairs={{0,4},{4,0},{1,5},{5,1},{2,6},{6,2},{3,7},{7,3},{8,12},{12,8},{9,1... | collective-permute-start | bytes 786440 | tf_op jit(solution)/shard_map/ppermute | solution.py:99
  9.6 6.5 %collective-permute-done.refs_1_ = f32[64,1024]{1,0:T(8,128)S(1)} collective-permute-done((f32[64,1024]{1,0:T(8,128)}, f32[64,1024]{1,0:T(8,128)S(1)}, u32[]{:S(2)}, u32[]{:S(2)}) %collective-permute-start) | collective-permute-done | bytes 262176 | tf_op jit(solution)/shard_map/ppermute | solution.py:99
  16.1 0.0 copy-start.6
  16.1 0.7 copy-done.6
  16.8 3.1 %shard_map.137 = (f32[16,64,128]{2,1,0:T(8,128)}, f32[16,64,128]{2,1,0:T(8,128)}) custom-call(s32[2]{0:T(128)} %pad_add_fusion.where_ref, bf16[2,256,64]{2,1,0:T(8,128)(2,1)} %constant.40.clone.high_ref, bf16[2,256,64]{2,1,0:T(8,128)(2,1)} %constant.41.clone.low_ref, f32[64,1024]{1,0:T(8,128)} %get-tuple-element.15.refs_0_, f32[64,1024]{1,0:T(8,128)} %copy-done.6), custom_call_target="tpu_custom_call" | custom-call | tf_op jit(solution)/shard_map/pallas_call | solution.py:47
  19.8 21.8 %all_to_all.20.refs_1_ = f32[16,64,128]{2,1,0:T(8,128)S(1)} all-to-all(f32[16,64,128]{2,1,0:T(8,128)} %get-tuple-element.18), channel_id=1, replica_groups=mesh['gx'=4,'gy'=2,'gz'=4] {'gx','gz'}, dimensions={0} | all-to-all | bytes 1048576 | tf_op jit(solution)/shard_map/all_to_all | solution.py:143
  41.6 0.0 copy-start
  41.6 3.6 %all-to-all-start = ((f32[16,64,128]{2,1,0:T(8,128)}), f32[16,64,128]{2,1,0:T(8,128)S(1)}, u32[]{:S(2)}, u32[]{:S(2)}) async-start(f32[16,64,128]{2,1,0:T(8,128)} %get-tuple-element.17), calls=%async_computation | async-start | bytes 1048576 | tf_op jit(solution)/shard_map/all_to_all | solution.py:143
  45.2 1.6 collective-permute-start.2
  46.7 14.0 %all-to-all-done.refs_0_ = f32[16,64,128]{2,1,0:T(8,128)S(1)} async-done(((f32[16,64,128]{2,1,0:T(8,128)}), f32[16,64,128]{2,1,0:T(8,128)S(1)}, u32[]{:S(2)}, u32[]{:S(2)}) %all-to-all-start) | async-done | bytes 524320 | tf_op jit(solution)/shard_map/all_to_all | solution.py:143
  60.7 0.0 copy-start.1
  60.7 1.5 collective-permute-start.1
  62.2 0.0 collective-permute-done.2.refs_3_
  62.2 0.0 copy-start.4
  62.2 12.0 %collective-permute-done.1.refs_2_ = f32[16,64,128]{2,1,0:T(8,128)S(1)} collective-permute-done((f32[16,64,128]{2,1,0:T(8,128)S(1)}, f32[16,64,128]{2,1,0:T(8,128)S(1)}, u32[]{:S(2)}, u32[]{:S(2)}) %collective-permute-start.1) | collective-permute-done | bytes 524320 | tf_op jit(solution)/shard_map/ppermute | solution.py:99
  74.3 0.0 copy-start.5
  74.3 0.0 copy-done
  74.3 0.0 copy-done.1
  74.3 0.0 copy-done.4
  74.3 0.8 copy-done.5
  75.1 12.5 %shard_map.138 = (f32[16,64,128]{2,1,0:T(8,128)}, f32[16,64,128]{2,1,0:T(8,128)}, f32[16,64,128]{2,1,0:T(8,128)}, f32[16,64,128]{2,1,0:T(8,128)}) custom-call(s32[2]{0:T(128)} %pad_add_fusion.where_ref, f32[8192,128]{1,0:T(8,128)} %bitcast.3, f32[8192,128]{1,0:T(8,128)} %bitcast.4, bf16[2,256,256]{2,1,0:T(8,128)(2,1)} %constant.42.clone.fzh, ...), custom_call_target="tpu_custom_call" | custom-call | tf_op jit(solution)/shard_map/pallas_call | solution.py:271
  87.6 0.0 copy-start.8
  87.6 0.0 copy-start.3
  87.6 1.6 collective-permute-start.3
  89.2 10.8 %collective-permute-done.3 = f32[16,64,128]{2,1,0:T(8,128)S(1)} collective-permute-done((f32[16,64,128]{2,1,0:T(8,128)}, f32[16,64,128]{2,1,0:T(8,128)S(1)}, u32[]{:S(2)}, u32[]{:S(2)}) %collective-permute-start.3) | collective-permute-done | bytes 524320 | tf_op jit(solution)/shard_map/ppermute | solution.py:99
  100.0 1.9 %add.10 = f32[16,64,128]{2,1,0:T(8,128)} add(f32[16,64,128]{2,1,0:T(8,128)} %get-tuple-element.19, f32[16,64,128]{2,1,0:T(8,128)S(1)} %collective-permute-done.3) | non-fusion elementwise | flops 131072 | bytes 1572864 | tf_op jit(solution)/shard_map/add | solution.py:288
  101.9 4.1 %all-to-all-start.2 = ((f32[16,64,128]{2,1,0:T(8,128)}), f32[16,64,128]{2,1,0:T(8,128)S(1)}, u32[]{:S(2)}, u32[]{:S(2)}) async-start(f32[16,64,128]{2,1,0:T(8,128)} %add.10), calls=%async_computation.2 | async-start | bytes 1048576 | tf_op jit(solution)/shard_map/all_to_all | solution.py:143
  106.1 0.0 copy-done.8
  106.1 1.6 collective-permute-start.4
  107.6 12.7 %collective-permute-done.4 = f32[16,64,128]{2,1,0:T(8,128)S(1)} collective-permute-done((f32[16,64,128]{2,1,0:T(8,128)S(1)}, f32[16,64,128]{2,1,0:T(8,128)S(1)}, u32[]{:S(2)}, u32[]{:S(2)}) %collective-permute-start.4) | collective-permute-done | bytes 524320 | tf_op jit(solution)/shard_map/ppermute | solution.py:99
  120.4 0.0 copy-done.3
  120.4 0.1 add.11
  120.5 1.2 all-to-all-done.2.re_ref
  121.6 0.0 copy-start.2
  121.6 20.0 %all_to_all.21.im_ref = f32[16,64,128]{2,1,0:T(8,128)} all-to-all(f32[16,64,128]{2,1,0:T(8,128)S(1)} %add.11), channel_id=1, replica_groups=mesh['gx'=4,'gy'=2,'gz'=4] {'gx','gz'}, dimensions={0} | all-to-all | bytes 1048576 | tf_op jit(solution)/shard_map/all_to_all | solution.py:143
  141.7 0.0 copy-done.2
  141.7 2.7 %shard_map.139 = (f32[64,1024]{1,0:T(8,128)}, f32[64,1024]{1,0:T(8,128)}) custom-call(s32[2]{0:T(128)} %pad_add_fusion.where_ref, bf16[2,64,256]{2,1,0:T(8,128)(2,1)} %constant.50.clone.high_ref, bf16[2,64,256]{2,1,0:T(8,128)(2,1)} %constant.51.clone.low_ref, f32[16,64,128]{2,1,0:T(8,128)} %copy-done.2, f32[16,64,128]{2,1,0:T(8,128)} %all_to_all.21.im_ref), custom_call_target="tpu_custom_call" | custom-call | tf_op jit(solution)/shard_map/pallas_call | solution.py:47
  144.3 1.5 collective-permute-start.5
  145.8 6.7 %collective-permute-done.5.refs_1_ = f32[64,1024]{1,0:T(8,128)S(1)} collective-permute-done((f32[64,1024]{1,0:T(8,128)}, f32[64,1024]{1,0:T(8,128)S(1)}, u32[]{:S(2)}, u32[]{:S(2)}) %collective-permute-start.5) | collective-permute-done | bytes 262176 | tf_op jit(solution)/shard_map/ppermute | solution.py:99
  152.5 0.0 copy-start.7
  152.5 0.7 copy-done.7
  153.2 2.8 %shard_map.140 = f32[64,64,32]{2,1,0:T(8,128)} custom-call(s32[2]{0:T(128)} %pad_add_fusion.where_ref, f32[64,1024]{1,0:T(8,128)} %get-tuple-element.23.refs_0_, f32[64,1024]{1,0:T(8,128)} %copy-done.7), custom_call_target="tpu_custom_call" | custom-call | tf_op jit(solution)/shard_map/pallas_call | solution.py:47
  156.1 3.2 %copy.16 = f32[64,64,32]{1,2,0:T(8,128)} copy(f32[64,64,32]{2,1,0:T(8,128)} %shard_map.140) | data formatting | bytes 1048576 | tf_op jit(solution)/shard_map/pallas_call | solution.py:47
Async XLA Ops:
  6.6 9.5 %collective-permute-start = (f32[64,1024]{1,0:T(8,128)}, f32[64,1024]{1,0:T(8,128)S(1)}, u32[]{:S(2)}, u32[]{:S(2)}) collective-permute-start(f32[64,1024]{1,0:T(8,128)} %get-tuple-element.16), channel_id=1, source_target_pairs={{0,4},{4,0},{1,5},{5,1},{2,6},{6,2},{3,7},{7,3},{8,12},{12,8},{9,1... | collective-permute-start | bytes 786440 | tf_op jit(solution)/shard_map/ppermute | solution.py:99
  16.1 0.7 copy-start.6
  41.6 32.7 %copy-start = (f32[16,64,128]{2,1,0:T(8,128)}, f32[16,64,128]{2,1,0:T(8,128)S(1)}, u32[]{:S(2)}) copy-start(f32[16,64,128]{2,1,0:T(8,128)S(1)} %all_to_all.20.refs_1_) | copy-start | bytes 1572868
  41.6 19.1 %all-to-all-start = ((f32[16,64,128]{2,1,0:T(8,128)}), f32[16,64,128]{2,1,0:T(8,128)S(1)}, u32[]{:S(2)}, u32[]{:S(2)}) async-start(f32[16,64,128]{2,1,0:T(8,128)} %get-tuple-element.17), calls=%async_computation | async-start | bytes 1048576 | tf_op jit(solution)/shard_map/all_to_all | solution.py:143
  45.2 17.0 %collective-permute-start.2 = (f32[16,64,128]{2,1,0:T(8,128)S(1)}, f32[16,64,128]{2,1,0:T(8,128)S(1)}, u32[]{:S(2)}, u32[]{:S(2)}) collective-permute-start(f32[16,64,128]{2,1,0:T(8,128)S(1)} %all_to_all.20.refs_1_), channel_id=1, source_target_pairs={{0,4},{4,0},{1,5},{5,1},{2,6},{6,2},{3,7},{7,3},{8,12},{12,8},{9,1... | collective-permute-start | bytes 1572872 | tf_op jit(solution)/shard_map/ppermute | solution.py:99
  60.7 13.5 %copy-start.1 = (f32[16,64,128]{2,1,0:T(8,128)}, f32[16,64,128]{2,1,0:T(8,128)S(1)}, u32[]{:S(2)}) copy-start(f32[16,64,128]{2,1,0:T(8,128)S(1)} %all-to-all-done.refs_0_) | copy-start | bytes 1572868
  60.7 13.5 %collective-permute-start.1 = (f32[16,64,128]{2,1,0:T(8,128)S(1)}, f32[16,64,128]{2,1,0:T(8,128)S(1)}, u32[]{:S(2)}, u32[]{:S(2)}) collective-permute-start(f32[16,64,128]{2,1,0:T(8,128)S(1)} %all-to-all-done.refs_0_), channel_id=1, source_target_pairs={{0,4},{4,0},{1,5},{5,1},{2,6},{6,2},{3,7},{7,3},{8,12},{12,8},{9,1... | collective-permute-start | bytes 1572872 | tf_op jit(solution)/shard_map/ppermute | solution.py:99
  62.2 12.1 %copy-start.4 = (f32[16,64,128]{2,1,0:T(8,128)}, f32[16,64,128]{2,1,0:T(8,128)S(1)}, u32[]{:S(2)}) copy-start(f32[16,64,128]{2,1,0:T(8,128)S(1)} %collective-permute-done.2.refs_3_) | copy-start | bytes 1572868
  74.3 0.8 copy-start.5
  87.6 18.5 %copy-start.8 = (f32[16,64,128]{2,1,0:T(8,128)S(1)}, f32[16,64,128]{2,1,0:T(8,128)}, u32[]{:S(2)}) copy-start(f32[16,64,128]{2,1,0:T(8,128)} %get-tuple-element.22) | copy-start | bytes 1572868
  87.6 32.8 %copy-start.3 = (f32[16,64,128]{2,1,0:T(8,128)S(1)}, f32[16,64,128]{2,1,0:T(8,128)}, u32[]{:S(2)}) copy-start(f32[16,64,128]{2,1,0:T(8,128)} %get-tuple-element.21) | copy-start | bytes 1572868
  87.6 12.4 %collective-permute-start.3 = (f32[16,64,128]{2,1,0:T(8,128)}, f32[16,64,128]{2,1,0:T(8,128)S(1)}, u32[]{:S(2)}, u32[]{:S(2)}) collective-permute-start(f32[16,64,128]{2,1,0:T(8,128)} %get-tuple-element.20), channel_id=1, source_target_pairs={{0,4},{4,0},{1,5},{5,1},{2,6},{6,2},{3,7},{7,3},{8,12},{12,8},{9,1... | collective-permute-start | bytes 1572872 | tf_op jit(solution)/shard_map/ppermute | solution.py:99
  101.9 19.7 %all-to-all-start.2 = ((f32[16,64,128]{2,1,0:T(8,128)}), f32[16,64,128]{2,1,0:T(8,128)S(1)}, u32[]{:S(2)}, u32[]{:S(2)}) async-start(f32[16,64,128]{2,1,0:T(8,128)} %add.10), calls=%async_computation.2 | async-start | bytes 1048576 | tf_op jit(solution)/shard_map/all_to_all | solution.py:143
  106.1 14.3 %collective-permute-start.4 = (f32[16,64,128]{2,1,0:T(8,128)S(1)}, f32[16,64,128]{2,1,0:T(8,128)S(1)}, u32[]{:S(2)}, u32[]{:S(2)}) collective-permute-start(f32[16,64,128]{2,1,0:T(8,128)S(1)} %copy-done.8), channel_id=1, source_target_pairs={{0,4},{4,0},{1,5},{5,1},{2,6},{6,2},{3,7},{7,3},{8,12},{12,8},{9,1... | collective-permute-start | bytes 1572872 | tf_op jit(solution)/shard_map/ppermute | solution.py:99
  121.6 20.0 %copy-start.2 = (f32[16,64,128]{2,1,0:T(8,128)}, f32[16,64,128]{2,1,0:T(8,128)S(1)}, u32[]{:S(2)}) copy-start(f32[16,64,128]{2,1,0:T(8,128)S(1)} %all-to-all-done.2.re_ref) | copy-start | bytes 1572868
  144.3 8.2 %collective-permute-start.5 = (f32[64,1024]{1,0:T(8,128)}, f32[64,1024]{1,0:T(8,128)S(1)}, u32[]{:S(2)}, u32[]{:S(2)}) collective-permute-start(f32[64,1024]{1,0:T(8,128)} %get-tuple-element.24), channel_id=1, source_target_pairs={{0,4},{4,0},{1,5},{5,1},{2,6},{6,2},{3,7},{7,3},{8,12},{12,8},{9,1... | collective-permute-start | bytes 786440 | tf_op jit(solution)/shard_map/ppermute | solution.py:99
  152.5 0.7 copy-start.7
where the time goes:
time: 160 us; the launch traced here: 159 us
  waiting for transfers between devices  64 us (40%)
  blocking collectives  41.8 us (26%)
  Pallas kernels  23.9 us (15%)
  starting transfers between devices  18.3 us (11%)
  local copies, waits for them, and re-layouts  8.54 us (5%)
  other arithmetic  2.63 us (2%)
    ppermute x6, waiting for transfers between devices, shift(): return lax.ppermute(value, 'gy', perm)  48.9 us
    all_to_all x2, blocking collectives, exchange(): return lax.all_to_all(value, ('gx', 'gz'), 0, 0, tiled=True)  41.8 us
    all_to_all x2, waiting for transfers between devices, exchange(): return lax.all_to_all(value, ('gx', 'gz'), 0, 0, tiled=True)  15.2 us
    pallas_call x1, Pallas kernels, per_device(): pl.pallas_call(middle_body, grid=(1,), out_shape=[plane] * (2 * size_gy),...  12.5 us
    pallas_call x4, Pallas kernels, call(): pl.pallas_call(body, out_shape=out_shape, in_specs=specs or [vmem] * len(...  11.3 us
    ppermute x6, starting transfers between devices, shift(): return lax.ppermute(value, 'gy', perm)  10.6 us
    all_to_all x2, starting transfers between devices, exchange(): return lax.all_to_all(value, ('gx', 'gz'), 0, 0, tiled=True)  7.71 us
    unnamed x19, local copies, waits for them, and re-layouts  5.39 us
  transfers between devices with their start and end apart: 8, of which 7 were waited for; matrix products, arithmetic and copies ran while one was open for 0% of the time, Pallas kernels for 0%

commit v1 on v0

--- a/solution.py
+++ b/solution.py
@@ -1,3 +1,4 @@
+import functools
 import math
 
 import jax
@@ -10,6 +11,7 @@
 
 LANES = 128
 SUBS = 8
+CHUNKS = 2
 
 
 def pair_frequency(length):
@@ -84,7 +86,8 @@
     per_tile = LANES // brick_z
     tiles_x = part_x // per_tile
     tiles_z = grid_z // LANES
-    rows_c = tiles_x * SUBS
+    sub = SUBS // CHUNKS
+    rows_c = tiles_x * sub
     count_k = long_z // size_gy
     units = grid_y
     f32 = jnp.float32
@@ -102,14 +105,13 @@
         for step in range(size_gy):
             base = (where_ref[0] + step) % size_gy * part_x
             for c in range(tiles_x):
-                outs[step][:, c * LANES : (c + 1) * LANES] = jnp.concatenate(
-                    [src_ref[base + c * per_tile + p] for p in range(per_tile)], axis=1
-                )
+                piece = src_ref[pl.ds(base + c * per_tile, per_tile)]
+                outs[step][:, c * LANES : (c + 1) * LANES] = piece.reshape(LANES, brick_y).T
 
     packed = call(
         pack_body,
         [jax.ShapeDtypeStruct((brick_y, tiles_x * LANES), f32)] * size_gy,
-        (where, source),
+        (where, jnp.swapaxes(source, 1, 2)),
         specs=[smem, vmem],
     )
     lines = [packed[0]] + [shift(packed[s], s) for s in range(1, size_gy)]
@@ -132,20 +134,18 @@
         for part in range(2):
             for c in range(tiles_x):
                 piece = total[part * units : (part + 1) * units, c * LANES : (c + 1) * LANES]
-                outs[part][:, c * SUBS : (c + 1) * SUBS, :] = piece.reshape(group, SUBS, LANES)
-
-    plane = jax.ShapeDtypeStruct((group, rows_c, LANES), f32)
+                piece = piece.reshape(group, SUBS, LANES)
+                at = part * rows_c + c * sub
+                for k in range(CHUNKS):
+                    outs[k][:, at : at + sub, :] = piece[:, k * sub : (k + 1) * sub]
+
+    plane = jax.ShapeDtypeStruct((group, 2 * rows_c, LANES), f32)
     spectra = call(
-        y_body, [plane] * 2, (where, *fwd_y, *lines), specs=[smem] + [vmem] * (2 + size_gy)
+        y_body, [plane] * CHUNKS, (where, *fwd_y, *lines), specs=[smem] + [vmem] * (2 + size_gy)
     )
 
     def exchange(value):
         return lax.all_to_all(value, ("gx", "gz"), 0, 0, tiled=True)
-
-    own = [exchange(v) for v in spectra]
-    gathered = list(own)
-    for s in range(1, size_gy):
-        gathered += [shift(v, s) for v in own]
 
     freq_z = pair_frequency(long_z).reshape(size_gy, count_k)
     fwd_z, inv_z = [], []
@@ -166,13 +166,15 @@
     fwd_x = split_table(np.concatenate([cos_x, sin_x], 0))
     inv_x = split_table(np.concatenate([cos_x * weight, sin_x * weight], 0).T)
     own_rows = green.shape[1]
-    green_rows = green.reshape(long_x * own_rows, count_k)
+    green_sub = own_rows // CHUNKS
     block_rows = per_tile * rows_c
 
-    def middle_body(where_ref, green_ref, edge_ref, fzh, fzl, izh, izl, fxh, fxl, ixh, ixl, *refs):
-        ins = refs[: 2 * size_gy]
-        outs = refs[2 * size_gy : 4 * size_gy]
-        field = refs[4 * size_gy]
+    def middle_body(
+        k, where_ref, green_ref, edge_ref, fzh, fzl, izh, izl, fxh, fxl, ixh, ixl, *refs
+    ):
+        ins = refs[:size_gy]
+        outs = refs[size_gy : 2 * size_gy]
+        field = refs[2 * size_gy]
         here = where_ref[0]
         is_first = where_ref[1] == 1
         table_z = (fzh[here], fzl[here])
@@ -182,12 +184,12 @@
             for g in range(size_gx):
                 cols = []
                 for part in range(2):
-                    ref = ins[2 * s + part]
+                    lo = part * rows_c
                     for t in range(tiles_z):
                         at = g * size_gz + t * per_tile
                         cols.append(
                             jnp.concatenate(
-                                block_transpose([ref[at + q] for q in range(per_tile)], brick_z), 0
+                                block_transpose([ins[s][at + q, lo : lo + rows_c] for q in range(per_tile)], brick_z), 0
                             )
                         )
                 rows = jnp.concatenate(cols, 1)
@@ -208,10 +210,10 @@
             both = mm((fxh[...], fxl[...]), halves(jnp.concatenate([re, im], 1)))
             cr, ci = both[:grid_x, :count_k], both[:grid_x, count_k:]
             sr, si = both[grid_x:, :count_k], both[grid_x:, count_k:]
-            gp = green_ref[pl.ds(row_p, grid_x, stride=own_rows), :]
-            gm = mirror(green_ref[pl.ds(row_m, grid_x, stride=own_rows), :])
+            gp = green_ref[:, row_p, :]
+            gm = mirror(green_ref[:, row_m, :])
             ga, gb = gp + gm, gp - gm
-            edge = edge_ref[pl.ds(row_p, 1), :] + mirror(edge_ref[pl.ds(row_m, 1), :])
+            edge = edge_ref[0, row_p : row_p + 1, :] + mirror(edge_ref[0, row_m : row_m + 1, :])
             top = lax.broadcasted_iota(jnp.int32, ga.shape, 0) == 0
             gb = jnp.where(top, 0.0, gb)
             ge = jnp.where(top, edge, ga)
@@ -219,10 +221,10 @@
             odd = jnp.concatenate([ge * sr - gb * ci, gb * cr + ge * si], 1)
             return mm((ixh[...], ixl[...]), halves(jnp.concatenate([even, odd], 0)))
 
-        for u in range(SUBS):
-            at_re = pl.ds(u, grid_x, stride=SUBS)
-            at_im = pl.ds(size_rows + u, grid_x, stride=SUBS)
-            if u == 0:
+        for u in range(sub):
+            at_re = pl.ds(u, grid_x, stride=sub)
+            at_im = pl.ds(size_rows + u, grid_x, stride=sub)
+            if u == 0 and k == 0:
 
                 @pl.when(is_first)
                 def _():
@@ -263,30 +265,39 @@
                             [col[p * rows_c : (p + 1) * rows_c] for p in range(per_tile)], brick_z
                         )
                         for q in range(per_tile):
-                            outs[2 * s + part][g * size_gz + t * per_tile + q] = pieces[q]
-
-    size_rows = grid_x * SUBS
-    operands = (where, green_rows, green_rows, *fwd_z, *inv_z, *fwd_x, *inv_x, *gathered)
+                            at = g * size_gz + t * per_tile + q
+                            outs[s][at, part * rows_c : (part + 1) * rows_c] = pieces[q]
+
+    size_rows = grid_x * sub
     whole = lambda value: pl.BlockSpec(value.shape, lambda i: (0,) * value.ndim)
-    returned = pl.pallas_call(
-        middle_body,
-        grid=(1,),
-        out_shape=[plane] * (2 * size_gy),
-        in_specs=[
-            smem,
-            pl.BlockSpec((grid_x * own_rows, count_k), lambda i: (0, 0)),
-            pl.BlockSpec((own_rows, count_k), lambda i: (grid_x, 0)),
-        ]
-        + [whole(v) for v in operands[3:]],
-        out_specs=[whole(plane)] * (2 * size_gy),
-        scratch_shapes=[pltpu.VMEM((2 * size_rows, count_k), f32)],
-        compiler_params=pltpu.CompilerParams(vmem_limit_bytes=56 * 2**20),
-    )(*operands)
-    summed = list(returned[:2])
-    for s in range(1, size_gy):
-        for part in range(2):
-            summed[part] = summed[part] + shift(returned[2 * s + part], size_gy - s)
-    last = [exchange(v) for v in summed]
+
+    def middle(k, gathered):
+        operands = (where, green, green, *fwd_z, *inv_z, *fwd_x, *inv_x, *gathered)
+        return pl.pallas_call(
+            functools.partial(middle_body, k),
+            grid=(1,),
+            out_shape=[plane] * size_gy,
+            in_specs=[
+                smem,
+                pl.BlockSpec((grid_x, green_sub, count_k), lambda i: (0, k, 0)),
+                pl.BlockSpec((1, green_sub, count_k), lambda i: (grid_x, k, 0)),
+            ]
+            + [whole(v) for v in operands[3:]],
+            out_specs=[whole(plane)] * size_gy,
+            scratch_shapes=[pltpu.VMEM((2 * size_rows, count_k), f32)],
+            compiler_params=pltpu.CompilerParams(vmem_limit_bytes=40 * 2**20),
+            name=f"middle{k}",
+        )(*operands)
+
+    last = []
+    own = [exchange(v) for v in spectra]
+    for k in range(CHUNKS):
+        gathered = [own[k]] + [shift(own[k], s) for s in range(1, size_gy)]
+        returned = middle(k, gathered)
+        summed = returned[0]
+        for s in range(1, size_gy):
+            summed = summed + shift(returned[s], size_gy - s)
+        last.append(exchange(summed))
 
     cos_b, sin_b = trig(np.arange(grid_y), np.arange(units), long_y)
     inv_re = 2.0 * cos_b
@@ -296,20 +307,17 @@
     inv_y = np.concatenate([inv_re, inv_im], 1) / long_y
     inv_y = split_table(inv_y.reshape(size_gy, brick_y, 2 * units))
 
-    def back_body(where_ref, high_ref, low_ref, re_ref, im_ref, *outs):
-        rows = jnp.concatenate(
-            [
-                jnp.concatenate(
-                    [
-                        ref[:, c * SUBS : (c + 1) * SUBS, :].reshape(units, LANES)
-                        for c in range(tiles_x)
-                    ],
-                    1,
-                )
-                for ref in (re_ref, im_ref)
-            ],
-            0,
-        )
+    def back_body(where_ref, high_ref, low_ref, *refs):
+        ins, outs = refs[:CHUNKS], refs[CHUNKS:]
+        cols = []
+        for c in range(tiles_x):
+            pieces = []
+            for part in range(2):
+                at = part * rows_c + c * sub
+                piece = jnp.concatenate([ref[:, at : at + sub, :] for ref in ins], 1)
+                pieces.append(piece.reshape(units, LANES))
+            cols.append(jnp.concatenate(pieces, 0))
+        rows = jnp.concatenate(cols, 1)
         rows = halves(rows)
         for s in range(size_gy):
             block = (where_ref[0] + s) % size_gy
@@ -319,7 +327,7 @@
         back_body,
         [jax.ShapeDtypeStruct((brick_y, tiles_x * LANES), f32)] * size_gy,
         (where, *inv_y, *last),
-        specs=[smem] + [vmem] * 4,
+        specs=[smem] + [vmem] * (2 + CHUNKS),
     )
     lines = [lines[0]] + [shift(lines[s], s) for s in range(1, size_gy)]
 
@@ -327,15 +335,19 @@
         ins, out = refs[:size_gy], refs[size_gy]
         for s in range(size_gy):
             base = (where_ref[0] + size_gy - s) % size_gy * part_x
-            for x in range(part_x):
-                out[base + x] = ins[s][:, x * brick_z : (x + 1) * brick_z]
-
-    return call(
+            for c in range(tiles_x):
+                piece = ins[s][:, c * LANES : (c + 1) * LANES].T
+                out[pl.ds(base + c * per_tile, per_tile)] = piece.reshape(
+                    per_tile, brick_z, brick_y
+                )
+
+    result = call(
         unpack_body,
-        jax.ShapeDtypeStruct(source.shape, f32),
+        jax.ShapeDtypeStruct((brick_x, brick_z, brick_y), f32),
         (where, *lines),
         specs=[smem] + [vmem] * size_gy,
     )
+    return jnp.swapaxes(result, 1, 2)
 
 
 def solution(mesh):

time: 160 us -> 150 us (0.938)
  waiting for transfers between devices: 64 us -> 47.4 us
  local copies, waits for them, and re-layouts: 8.54 us -> 16.7 us
  Pallas kernels: 23.9 us -> 21.9 us
    all_to_all x2, waiting for transfers between devices: 15.2 us -> 0.01 us  [exchange(): return lax.all_to_all(value, ('gx', 'gz'), 0, 0, tiled=True)]
    unnamed x19 -> x50, local copies, waits for them, and re-layouts: 5.39 us -> 16.7 us
    pallas_call x1 -> x0, local copies, waits for them, and re-layouts: 3.16 us -> none  [call(): pl.pallas_call(body, out_shape=out_shape, in_specs=specs or [vmem] * len(...]
    pallas_call x1 -> x2, Pallas kernels: 12.5 us -> 11.5 us  [middle(): pl.pallas_call(functools.partial(middle_body, k), grid=(1,), out_shape=[p...]
  transfers between devices with their start and end apart: 8 -> 8, of which waited for: 7 -> 6; matrix products, arithmetic and copies ran while one was open for 0% -> 1% of each run, Pallas kernels for 0% -> 8%
where the time goes in v1:
time: 150 us; the launch traced here: 149 us
  waiting for transfers between devices  47.4 us (32%)
  blocking collectives  42.4 us (28%)
  Pallas kernels  21.9 us (15%)
  starting transfers between devices  17.4 us (12%)
  local copies, waits for them, and re-layouts  16.7 us (11%)
  other arithmetic  2.79 us (2%)
    ppermute x6, waiting for transfers between devices, shift(): return lax.ppermute(value, 'gy', perm)  47.4 us
    all_to_all x2, blocking collectives, exchange(): return lax.all_to_all(value, ('gx', 'gz'), 0, 0, tiled=True)  42.4 us
    unnamed x50, local copies, waits for them, and re-layouts  16.7 us
    pallas_call x2, Pallas kernels, middle(): pl.pallas_call(functools.partial(middle_body, k), grid=(1,), out_shape=[p...  11.5 us
    pallas_call x4, Pallas kernels, call(): pl.pallas_call(body, out_shape=out_shape, in_specs=specs or [vmem] * len(...  10.4 us
    ppermute x6, starting transfers between devices, shift(): return lax.ppermute(value, 'gy', perm)  9.57 us
    all_to_all x2, starting transfers between devices, exchange(): return lax.all_to_all(value, ('gx', 'gz'), 0, 0, tiled=True)  7.81 us
  transfers between devices with their start and end apart: 8, of which 6 were waited for; matrix products, arithmetic and copies ran while one was open for 1% of the time, Pallas kernels for 8%

profile of v1, /device:TPU:0, one launch (start us, length us, event | category | flops | bytes accessed | tf_op | source)
XLA Modules:
  0.0 148.8 jit_solution(12566465454912605650)
XLA Ops:
  0.0 0.7 pad_add_fusion.where_ref
  0.7 2.3 %shard_map.136 = (f32[64,1024]{1,0:T(8,128)}, f32[64,1024]{1,0:T(8,128)}) custom-call(s32[2]{0:T(128)} %pad_add_fusion.where_ref, f32[64,32,64]{2,1,0:T(8,128)} %bitcast.4), custom_call_target="tpu_custom_call" | custom-call | tf_op jit(solution)/shard_map/pallas_call | solution.py:49
  2.9 3.0 %collective-permute-start = (f32[64,1024]{1,0:T(8,128)}, f32[64,1024]{1,0:T(8,128)S(1)}, u32[]{:S(2)}, u32[]{:S(2)}) collective-permute-start(f32[64,1024]{1,0:T(8,128)} %get-tuple-element.16), channel_id=1, source_target_pairs={{0,4},{4,0},{1,5},{5,1},{2,6},{6,2},{3,7},{7,3},{8,12},{12,8},{9,1... | collective-permute-start | bytes 786440 | tf_op jit(solution)/shard_map/ppermute | solution.py:102
  5.9 6.5 %collective-permute-done.refs_1_ = f32[64,1024]{1,0:T(8,128)S(1)} collective-permute-done((f32[64,1024]{1,0:T(8,128)}, f32[64,1024]{1,0:T(8,128)S(1)}, u32[]{:S(2)}, u32[]{:S(2)}) %collective-permute-start) | collective-permute-done | bytes 262176 | tf_op jit(solution)/shard_map/ppermute | solution.py:102
  12.4 0.0 copy-start.23
  12.4 0.7 copy-done.23
  13.1 3.1 %shard_map.137 = (f32[16,64,128]{2,1,0:T(8,128)}, f32[16,64,128]{2,1,0:T(8,128)}) custom-call(s32[2]{0:T(128)} %pad_add_fusion.where_ref, bf16[2,256,64]{2,1,0:T(8,128)(2,1)} %constant.40.clone.high_ref, bf16[2,256,64]{2,1,0:T(8,128)(2,1)} %constant.41.clone.low_ref, f32[64,1024]{1,0:T(8,128)} %get-tuple-element.15.refs_0_, f32[64,1024]{1,0:T(8,128)} %copy-done.23), custom_call_target="tpu_custom_call" | custom-call | tf_op jit(solution)/shard_map/pallas_call | solution.py:49
  16.2 21.7 %all_to_all.20.refs_0_ = f32[16,64,128]{2,1,0:T(8,128)S(1)} all-to-all(f32[16,64,128]{2,1,0:T(8,128)} %get-tuple-element.20), channel_id=1, replica_groups=mesh['gx'=4,'gy'=2,'gz'=4] {'gx','gz'}, dimensions={0} | all-to-all | bytes 1048576 | tf_op jit(solution)/shard_map/all_to_all | solution.py:148
  37.9 1.5 %collective-permute-start.3 = (f32[16,64,128]{2,1,0:T(8,128)S(1)}, f32[16,64,128]{2,1,0:T(8,128)S(1)}, u32[]{:S(2)}, u32[]{:S(2)}) collective-permute-start(f32[16,64,128]{2,1,0:T(8,128)S(1)} %all_to_all.20.refs_0_), channel_id=1, source_target_pairs={{0,4},{4,0},{1,5},{5,1},{2,6},{6,2},{3,7},{7,3},{8,12},{12,8},{9,1... | collective-permute-start | bytes 1572872 | tf_op jit(solution)/shard_map/ppermute | solution.py:102
  39.4 3.6 %all-to-all-start = ((f32[16,64,128]{2,1,0:T(8,128)}), f32[16,64,128]{2,1,0:T(8,128)S(1)}, u32[]{:S(2)}, u32[]{:S(2)}) async-start(f32[16,64,128]{2,1,0:T(8,128)} %get-tuple-element.17), calls=%async_computation | async-start | bytes 1048576 | tf_op jit(solution)/shard_map/all_to_all | solution.py:148
  43.0 8.5 %collective-permute-done.3.refs_1_ = f32[16,64,128]{2,1,0:T(8,128)S(1)} collective-permute-done((f32[16,64,128]{2,1,0:T(8,128)S(1)}, f32[16,64,128]{2,1,0:T(8,128)S(1)}, u32[]{:S(2)}, u32[]{:S(2)}) %collective-permute-start.3) | collective-permute-done | bytes 524320 | tf_op jit(solution)/shard_map/ppermute | solution.py:102
  51.5 0.0 copy-start.19
  51.5 0.8 copy-done.19
  52.3 0.0 copy-start
  52.3 2.2 %copy-done = f32[512,16,128]{2,1,0:T(8,128)S(1)} copy-done((f32[512,16,128]{2,1,0:T(8,128)S(1)}, f32[512,16,128]{2,1,0:T(8,128)}, u32[]{:S(2)}) %copy-start) | copy-done | bytes 4194328
  54.5 0.0 copy-start.2
  54.5 0.9 copy-done.2
  55.5 0.0 copy-start.4
  55.5 0.9 copy-done.4
  56.4 0.0 copy-start.6
  56.4 0.9 copy-done.6
  57.4 0.9 copy-done.8
  58.3 0.9 copy-done.10
  59.3 0.9 copy-done.12
  60.2 0.9 copy-done.14
  61.2 0.9 copy-done.16
  62.1 1.0 copy-done.20
  63.2 0.7 copy-done.21
  63.8 0.0 copy-start.11
  63.8 0.0 copy-start.13
  63.9 0.0 copy-start.15
  63.9 0.0 copy-start.17
  63.9 0.0 copy-start.22
  63.9 5.5 %middle1.1 = (f32[16,64,128]{2,1,0:T(8,128)S(1)}, f32[16,64,128]{2,1,0:T(8,128)}) custom-call(s32[2]{0:T(128)S(1)} %copy-done.21, f32[512,16,128]{2,1,0:T(8,128)S(1)} %copy-done, f32[512,16,128]{2,1,0:T(8,128)S(1)} %copy-done, bf16[2,256,256]{2,1,0:T(8,128)(2,1)S(1)} %copy-done.16, bf16[2,256,256]{2,1,0:T(8,128)(2,1)S(1)} %copy-done.14, ...), custom_call_target="tpu_custom_call" | custom-call | tf_op jit(solution)/shard_map/middle1/pallas_call | solution.py:276
  69.4 0.8 copy-done.18
  70.3 1.5 %collective-permute-start.4 = (f32[16,64,128]{2,1,0:T(8,128)}, f32[16,64,128]{2,1,0:T(8,128)}, u32[]{:S(2)}, u32[]{:S(2)}) collective-permute-start(f32[16,64,128]{2,1,0:T(8,128)} %get-tuple-element.22), channel_id=1, source_target_pairs={{0,4},{4,0},{1,5},{5,1},{2,6},{6,2},{3,7},{7,3},{8,12},{12,8},{9,1... | collective-permute-start | bytes 1572872 | tf_op jit(solution)/shard_map/ppermute | solution.py:102
  71.8 0.0 all-to-all-done.refs_0_
  71.8 0.5 collective-permute-start.1
  72.3 13.1 %collective-permute-done.4 = f32[16,64,128]{2,1,0:T(8,128)} collective-permute-done((f32[16,64,128]{2,1,0:T(8,128)}, f32[16,64,128]{2,1,0:T(8,128)}, u32[]{:S(2)}, u32[]{:S(2)}) %collective-permute-start.4) | collective-permute-done | bytes 524320 | tf_op jit(solution)/shard_map/ppermute | solution.py:102
  85.4 2.1 %add.11 = f32[16,64,128]{2,1,0:T(8,128)} add(f32[16,64,128]{2,1,0:T(8,128)} %copy-done.18, f32[16,64,128]{2,1,0:T(8,128)} %collective-permute-done.4) | non-fusion elementwise | flops 131072 | bytes 1572864 | tf_op jit(solution)/shard_map/add | solution.py:299
  87.4 4.2 %all-to-all-start.3 = ((f32[16,64,128]{2,1,0:T(8,128)}), f32[16,64,128]{2,1,0:T(8,128)}, u32[]{:S(2)}, u32[]{:S(2)}) async-start(f32[16,64,128]{2,1,0:T(8,128)} %add.11), calls=%async_computation.3 | async-start | bytes 1048576 | tf_op jit(solution)/shard_map/all_to_all | solution.py:148
  91.7 2.8 %collective-permute-done.1.refs_1_ = f32[16,64,128]{2,1,0:T(8,128)S(1)} collective-permute-done((f32[16,64,128]{2,1,0:T(8,128)S(1)}, f32[16,64,128]{2,1,0:T(8,128)S(1)}, u32[]{:S(2)}, u32[]{:S(2)}) %collective-permute-start.1) | collective-permute-done | bytes 524320 | tf_op jit(solution)/shard_map/ppermute | solution.py:102
  94.5 0.0 copy-done.3
  94.5 0.0 copy-done.5
  94.5 0.0 copy-done.7
  94.5 0.0 copy-done.9
  94.5 0.0 copy-done.11
  94.5 0.0 copy-done.13
  94.5 0.0 copy-done.15
  94.5 0.0 copy-done.17
  94.5 0.0 copy-done.22
  94.5 0.0 copy-start.1
  94.5 2.2 %copy-done.1 = f32[512,16,128]{2,1,0:T(8,128)S(1)} copy-done((f32[512,16,128]{2,1,0:T(8,128)S(1)}, f32[512,16,128]{2,1,0:T(8,128)}, u32[]{:S(2)}) %copy-start.1) | copy-done | bytes 4194328
  96.7 5.9 %middle0.1 = (f32[16,64,128]{2,1,0:T(8,128)S(1)}, f32[16,64,128]{2,1,0:T(8,128)S(1)}) custom-call(s32[2]{0:T(128)S(1)} %copy-done.22, f32[512,16,128]{2,1,0:T(8,128)S(1)} %copy-done.1, f32[512,16,128]{2,1,0:T(8,128)S(1)} %copy-done.1, bf16[2,256,256]{2,1,0:T(8,128)(2,1)S(1)} %copy-done.17, bf16[2,256,256]{2,1,0:T(8,128)(2,1)S(1)} %copy-done.15, ...), custom_call_target="tpu_custom_call" | custom-call | tf_op jit(solution)/shard_map/middle0/pallas_call | solution.py:276
  102.7 1.6 %collective-permute-start.2 = (f32[16,64,128]{2,1,0:T(8,128)S(1)}, f32[16,64,128]{2,1,0:T(8,128)S(1)}, u32[]{:S(2)}, u32[]{:S(2)}) collective-permute-start(f32[16,64,128]{2,1,0:T(8,128)S(1)} %get-tuple-element.19), channel_id=1, source_target_pairs={{0,4},{4,0},{1,5},{5,1},{2,6},{6,2},{3,7},{7,3},{8,12},{12,8},{9,1... | collective-permute-start | bytes 1572872 | tf_op jit(solution)/shard_map/ppermute | solution.py:102
  104.2 9.8 %collective-permute-done.2 = f32[16,64,128]{2,1,0:T(8,128)S(1)} collective-permute-done((f32[16,64,128]{2,1,0:T(8,128)S(1)}, f32[16,64,128]{2,1,0:T(8,128)S(1)}, u32[]{:S(2)}, u32[]{:S(2)}) %collective-permute-start.2) | collective-permute-done | bytes 524320 | tf_op jit(solution)/shard_map/ppermute | solution.py:102
  114.0 0.1 add.10
  114.1 0.0 all-to-all-done.3.refs_1_
  114.1 20.7 %all_to_all.21.refs_0_ = f32[16,64,128]{2,1,0:T(8,128)} all-to-all(f32[16,64,128]{2,1,0:T(8,128)S(1)} %add.10), channel_id=1, replica_groups=mesh['gx'=4,'gy'=2,'gz'=4] {'gx','gz'}, dimensions={0} | all-to-all | bytes 1048576 | tf_op jit(solution)/shard_map/all_to_all | solution.py:148
  134.8 2.7 %shard_map.138 = (f32[64,1024]{1,0:T(8,128)}, f32[64,1024]{1,0:T(8,128)}) custom-call(s32[2]{0:T(128)} %pad_add_fusion.where_ref, bf16[2,64,256]{2,1,0:T(8,128)(2,1)} %constant.50.clone.high_ref, bf16[2,64,256]{2,1,0:T(8,128)(2,1)} %constant.51.clone.low_ref, f32[16,64,128]{2,1,0:T(8,128)} %all_to_all.21.refs_0_, f32[16,64,128]{2,1,0:T(8,128)} %all-to-all-done.3.refs_1_), custom_call_target="tpu_custom_call" | custom-call | tf_op jit(solution)/shard_map/pallas_call | solution.py:49
  137.5 1.5 %collective-permute-start.5 = (f32[64,1024]{1,0:T(8,128)}, f32[64,1024]{1,0:T(8,128)S(1)}, u32[]{:S(2)}, u32[]{:S(2)}) collective-permute-start(f32[64,1024]{1,0:T(8,128)} %get-tuple-element.24), channel_id=1, source_target_pairs={{0,4},{4,0},{1,5},{5,1},{2,6},{6,2},{3,7},{7,3},{8,12},{12,8},{9,1... | collective-permute-start | bytes 786440 | tf_op jit(solution)/shard_map/ppermute | solution.py:102
  139.0 6.7 %collective-permute-done.5.refs_1_ = f32[64,1024]{1,0:T(8,128)S(1)} collective-permute-done((f32[64,1024]{1,0:T(8,128)}, f32[64,1024]{1,0:T(8,128)S(1)}, u32[]{:S(2)}, u32[]{:S(2)}) %collective-permute-start.5) | collective-permute-done | bytes 262176 | tf_op jit(solution)/shard_map/ppermute | solution.py:102
  145.7 0.7 copy-done.24
  146.4 2.3 %shard_map.139 = f32[64,32,64]{2,1,0:T(8,128)} custom-call(s32[2]{0:T(128)} %pad_add_fusion.where_ref, f32[64,1024]{1,0:T(8,128)} %get-tuple-element.23.refs_0_, f32[64,1024]{1,0:T(8,128)} %copy-done.24), custom_call_target="tpu_custom_call" | custom-call | tf_op jit(solution)/shard_map/pallas_call | solution.py:49
  (13 shorter events, 0.0 us)
Async XLA Ops:
  2.9 9.5 %collective-permute-start = (f32[64,1024]{1,0:T(8,128)}, f32[64,1024]{1,0:T(8,128)S(1)}, u32[]{:S(2)}, u32[]{:S(2)}) collective-permute-start(f32[64,1024]{1,0:T(8,128)} %get-tuple-element.16), channel_id=1, source_target_pairs={{0,4},{4,0},{1,5},{5,1},{2,6},{6,2},{3,7},{7,3},{8,12},{12,8},{9,1... | collective-permute-start | bytes 786440 | tf_op jit(solution)/shard_map/ppermute | solution.py:102
  12.4 0.7 copy-start.23
  37.9 13.6 %collective-permute-start.3 = (f32[16,64,128]{2,1,0:T(8,128)S(1)}, f32[16,64,128]{2,1,0:T(8,128)S(1)}, u32[]{:S(2)}, u32[]{:S(2)}) collective-permute-start(f32[16,64,128]{2,1,0:T(8,128)S(1)} %all_to_all.20.refs_0_), channel_id=1, source_target_pairs={{0,4},{4,0},{1,5},{5,1},{2,6},{6,2},{3,7},{7,3},{8,12},{12,8},{9,1... | collective-permute-start | bytes 1572872 | tf_op jit(solution)/shard_map/ppermute | solution.py:102
  39.4 32.3 %all-to-all-start = ((f32[16,64,128]{2,1,0:T(8,128)}), f32[16,64,128]{2,1,0:T(8,128)S(1)}, u32[]{:S(2)}, u32[]{:S(2)}) async-start(f32[16,64,128]{2,1,0:T(8,128)} %get-tuple-element.17), calls=%async_computation | async-start | bytes 1048576 | tf_op jit(solution)/shard_map/all_to_all | solution.py:148
  51.5 0.8 copy-start.19
  52.3 2.2 %copy-start = (f32[512,16,128]{2,1,0:T(8,128)S(1)}, f32[512,16,128]{2,1,0:T(8,128)}, u32[]{:S(2)}) copy-start(f32[512,16,128]{2,1,0:T(8,128)} %edge_ref.3) | copy-start | bytes 12582916
  54.5 0.9 copy-start.2
  55.5 0.9 copy-start.4
  56.4 0.9 copy-start.6
  57.4 0.9 copy-start.8
  58.3 0.9 copy-start.10
  59.3 0.9 copy-start.12
  60.2 0.9 copy-start.14
  61.2 0.9 copy-start.16
  62.1 1.0 copy-start.20
  63.2 0.7 copy-start.21
  63.8 30.6 %copy-start.3 = (bf16[256,512]{1,0:T(8,128)(2,1)S(1)}, bf16[256,512]{1,0:T(8,128)(2,1)}, u32[]{:S(2)}) copy-start(bf16[256,512]{1,0:T(8,128)(2,1)} %constant.49.clone.ixl) | copy-start | bytes 786436
  63.8 30.6 %copy-start.5 = (bf16[256,512]{1,0:T(8,128)(2,1)S(1)}, bf16[256,512]{1,0:T(8,128)(2,1)}, u32[]{:S(2)}) copy-start(bf16[256,512]{1,0:T(8,128)(2,1)} %constant.48.clone.ixh) | copy-start | bytes 786436
  63.8 30.6 %copy-start.7 = (bf16[512,256]{1,0:T(8,128)(2,1)S(1)}, bf16[512,256]{1,0:T(8,128)(2,1)}, u32[]{:S(2)}) copy-start(bf16[512,256]{1,0:T(8,128)(2,1)} %constant.47.clone.fxl) | copy-start | bytes 786436
  63.8 30.6 %copy-start.9 = (bf16[512,256]{1,0:T(8,128)(2,1)S(1)}, bf16[512,256]{1,0:T(8,128)(2,1)}, u32[]{:S(2)}) copy-start(bf16[512,256]{1,0:T(8,128)(2,1)} %constant.46.clone.fxh) | copy-start | bytes 786436
  63.8 30.6 %copy-start.11 = (bf16[2,256,256]{2,1,0:T(8,128)(2,1)S(1)}, bf16[2,256,256]{2,1,0:T(8,128)(2,1)}, u32[]{:S(2)}) copy-start(bf16[2,256,256]{2,1,0:T(8,128)(2,1)} %constant.45.clone.izl) | copy-start | bytes 786436
  63.8 30.6 %copy-start.13 = (bf16[2,256,256]{2,1,0:T(8,128)(2,1)S(1)}, bf16[2,256,256]{2,1,0:T(8,128)(2,1)}, u32[]{:S(2)}) copy-start(bf16[2,256,256]{2,1,0:T(8,128)(2,1)} %constant.44.clone.izh) | copy-start | bytes 786436
  63.9 30.6 %copy-start.15 = (bf16[2,256,256]{2,1,0:T(8,128)(2,1)S(1)}, bf16[2,256,256]{2,1,0:T(8,128)(2,1)}, u32[]{:S(2)}) copy-start(bf16[2,256,256]{2,1,0:T(8,128)(2,1)} %constant.43.clone.fzl) | copy-start | bytes 786436
  63.9 30.6 %copy-start.17 = (bf16[2,256,256]{2,1,0:T(8,128)(2,1)S(1)}, bf16[2,256,256]{2,1,0:T(8,128)(2,1)}, u32[]{:S(2)}) copy-start(bf16[2,256,256]{2,1,0:T(8,128)(2,1)} %constant.42.clone.fzh) | copy-start | bytes 786436
  63.9 30.6 %copy-start.22 = (s32[2]{0:T(128)S(1)}, s32[2]{0:T(128)}, u32[]{:S(2)}) copy-start(s32[2]{0:T(128)} %pad_add_fusion.where_ref) | copy-start | bytes 28
  69.4 0.8 copy-start.18
  70.3 15.1 %collective-permute-start.4 = (f32[16,64,128]{2,1,0:T(8,128)}, f32[16,64,128]{2,1,0:T(8,128)}, u32[]{:S(2)}, u32[]{:S(2)}) collective-permute-start(f32[16,64,128]{2,1,0:T(8,128)} %get-tuple-element.22), channel_id=1, source_target_pairs={{0,4},{4,0},{1,5},{5,1},{2,6},{6,2},{3,7},{7,3},{8,12},{12,8},{9,1... | collective-permute-start | bytes 1572872 | tf_op jit(solution)/shard_map/ppermute | solution.py:102
  71.8 22.7 %collective-permute-start.1 = (f32[16,64,128]{2,1,0:T(8,128)S(1)}, f32[16,64,128]{2,1,0:T(8,128)S(1)}, u32[]{:S(2)}, u32[]{:S(2)}) collective-permute-start(f32[16,64,128]{2,1,0:T(8,128)S(1)} %all-to-all-done.refs_0_), channel_id=1, source_target_pairs={{0,4},{4,0},{1,5},{5,1},{2,6},{6,2},{3,7},{7,3},{8,12},{12,8},{9,1... | collective-permute-start | bytes 1572872 | tf_op jit(solution)/shard_map/ppermute | solution.py:102
  87.4 26.7 %all-to-all-start.3 = ((f32[16,64,128]{2,1,0:T(8,128)}), f32[16,64,128]{2,1,0:T(8,128)}, u32[]{:S(2)}, u32[]{:S(2)}) async-start(f32[16,64,128]{2,1,0:T(8,128)} %add.11), calls=%async_computation.3 | async-start | bytes 1048576 | tf_op jit(solution)/shard_map/all_to_all | solution.py:148
  94.5 2.2 %copy-start.1 = (f32[512,16,128]{2,1,0:T(8,128)S(1)}, f32[512,16,128]{2,1,0:T(8,128)}, u32[]{:S(2)}) copy-start(f32[512,16,128]{2,1,0:T(8,128)} %edge_ref.3) | copy-start | bytes 12582916
  102.7 11.4 %collective-permute-start.2 = (f32[16,64,128]{2,1,0:T(8,128)S(1)}, f32[16,64,128]{2,1,0:T(8,128)S(1)}, u32[]{:S(2)}, u32[]{:S(2)}) collective-permute-start(f32[16,64,128]{2,1,0:T(8,128)S(1)} %get-tuple-element.19), channel_id=1, source_target_pairs={{0,4},{4,0},{1,5},{5,1},{2,6},{6,2},{3,7},{7,3},{8,12},{12,8},{9,1... | collective-permute-start | bytes 1572872 | tf_op jit(solution)/shard_map/ppermute | solution.py:102
  137.5 8.2 %collective-permute-start.5 = (f32[64,1024]{1,0:T(8,128)}, f32[64,1024]{1,0:T(8,128)S(1)}, u32[]{:S(2)}, u32[]{:S(2)}) collective-permute-start(f32[64,1024]{1,0:T(8,128)} %get-tuple-element.24), channel_id=1, source_target_pairs={{0,4},{4,0},{1,5},{5,1},{2,6},{6,2},{3,7},{7,3},{8,12},{12,8},{9,1... | collective-permute-start | bytes 786440 | tf_op jit(solution)/shard_map/ppermute | solution.py:102
  145.7 0.7 copy-start.24

commit v2 on v1

--- a/solution.py
+++ b/solution.py
@@ -30,7 +30,7 @@
     table = np.asarray(table, np.float32)
     high = table.astype(jnp.bfloat16)
     low = (table - high.astype(np.float32)).astype(jnp.bfloat16)
-    return jnp.asarray(high), jnp.asarray(low)
+    return high, low
 
 
 def halves(value):
@@ -52,7 +52,7 @@
         in_specs=specs or [vmem] * len(operands),
         out_specs=jax.tree.map(lambda _: vmem, out_shape),
         scratch_shapes=list(scratch),
-        compiler_params=pltpu.CompilerParams(vmem_limit_bytes=56 * 2**20),
+        compiler_params=pltpu.CompilerParams(vmem_limit_bytes=40 * 2**20),
     )(*operands)
 
 
@@ -122,7 +122,7 @@
     im_y[0] = sign_y
     fwd_y = np.concatenate([cos_y, im_y], 0)
     fwd_y = fwd_y.reshape(2 * units, size_gy, brick_y).transpose(1, 0, 2)
-    fwd_y = split_table(fwd_y)
+    fwd_y = [jnp.asarray(v) for v in split_table(fwd_y)]
 
     def y_body(where_ref, high_ref, low_ref, *refs):
         ins, outs = refs[:size_gy], refs[size_gy:]
@@ -169,16 +169,49 @@
     green_sub = own_rows // CHUNKS
     block_rows = per_tile * rows_c
 
-    def middle_body(
-        k, where_ref, green_ref, edge_ref, fzh, fzl, izh, izl, fxh, fxl, ixh, ixl, *refs
-    ):
+    width = 2 * LANES
+    pieces, starts, at_row = [], {}, 0
+    for name, pair in (("fz", fwd_z), ("iz", inv_z), ("fx", fwd_x), ("ix", inv_x)):
+        for level in range(2):
+            value = pair[level]
+            value = value.reshape((-1,) + value.shape[-2:])
+            starts[name, level] = (at_row, value.shape[1], value.shape[2] // width)
+            for block in range(value.shape[0]):
+                for col in range(0, value.shape[2], width):
+                    pieces.append(value[block, :, col : col + width])
+                    at_row += value.shape[1]
+    tables = jnp.asarray(np.concatenate(pieces, 0))
+
+    def middle_body(k, where_ref, green_hbm, table_ref, *refs):
         ins = refs[:size_gy]
         outs = refs[size_gy : 2 * size_gy]
-        field = refs[2 * size_gy]
+        field, green_ref, edge_ref, sems = refs[2 * size_gy :]
+        part_k = pl.ds(k * green_sub, green_sub)
+        copies = [
+            pltpu.make_async_copy(
+                green_hbm.at[pl.ds(0, grid_x), part_k, :], green_ref, sems.at[0]
+            ),
+            pltpu.make_async_copy(
+                green_hbm.at[pl.ds(grid_x, 1), part_k, :], edge_ref, sems.at[1]
+            ),
+        ]
+        for copy in copies:
+            copy.start()
+
+        def table(name, block=0):
+            levels = []
+            for level in range(2):
+                start, rows, cols = starts[name, level]
+                base = start + block * (rows * cols)
+                if not isinstance(block, int):
+                    base = pl.multiple_of(base, 2 * SUBS)
+                parts = [table_ref[pl.ds(base + c * rows, rows), :] for c in range(cols)]
+                levels.append(parts[0] if cols == 1 else jnp.concatenate(parts, 1))
+            return levels
+
         here = where_ref[0]
         is_first = where_ref[1] == 1
-        table_z = (fzh[here], fzl[here])
-        back_z = (izh[here], izl[here])
+        table_z = table("fz", here)
         for s in range(size_gy):
             side = (here + size_gy - s) % size_gy
             for g in range(size_gx):
@@ -198,6 +231,9 @@
                 field[pl.ds(offset, block_rows), :] = out[:, :count_k]
                 field[pl.ds(size_rows + offset, block_rows), :] = out[:, count_k:]
 
+        for copy in copies:
+            copy.wait()
+
         def mirror(value):
             lane = lax.broadcasted_iota(jnp.int32, value.shape, 1)
             swapped = jnp.where(
@@ -207,7 +243,7 @@
             return jnp.where(keep, value, swapped)
 
         def filtered(re, im, row_p, row_m):
-            both = mm((fxh[...], fxl[...]), halves(jnp.concatenate([re, im], 1)))
+            both = mm(table("fx"), halves(jnp.concatenate([re, im], 1)))
             cr, ci = both[:grid_x, :count_k], both[:grid_x, count_k:]
             sr, si = both[grid_x:, :count_k], both[grid_x:, count_k:]
             gp = green_ref[:, row_p, :]
@@ -219,7 +255,7 @@
             ge = jnp.where(top, edge, ga)
             even = jnp.concatenate([ga * cr + gb * si, ga * ci - gb * sr], 1)
             odd = jnp.concatenate([ge * sr - gb * ci, gb * cr + ge * si], 1)
-            return mm((ixh[...], ixl[...]), halves(jnp.concatenate([even, odd], 0)))
+            return mm(table("ix"), halves(jnp.concatenate([even, odd], 0)))
 
         for u in range(sub):
             at_re = pl.ds(u, grid_x, stride=sub)
@@ -245,6 +281,7 @@
                 field[at_re, :] = out[:, :count_k]
                 field[at_im, :] = out[:, count_k:]
 
+        back_z = table("iz", here)
         for s in range(size_gy):
             side = (here + size_gy - s) % size_gy
             for g in range(size_gx):
@@ -269,25 +306,20 @@
                             outs[s][at, part * rows_c : (part + 1) * rows_c] = pieces[q]
 
     size_rows = grid_x * sub
-    whole = lambda value: pl.BlockSpec(value.shape, lambda i: (0,) * value.ndim)
-
+    hbm = pl.BlockSpec(memory_space=pltpu.HBM)
     def middle(k, gathered):
-        operands = (where, green, green, *fwd_z, *inv_z, *fwd_x, *inv_x, *gathered)
-        return pl.pallas_call(
+        return call(
             functools.partial(middle_body, k),
-            grid=(1,),
-            out_shape=[plane] * size_gy,
-            in_specs=[
-                smem,
-                pl.BlockSpec((grid_x, green_sub, count_k), lambda i: (0, k, 0)),
-                pl.BlockSpec((1, green_sub, count_k), lambda i: (grid_x, k, 0)),
-            ]
-            + [whole(v) for v in operands[3:]],
-            out_specs=[whole(plane)] * size_gy,
-            scratch_shapes=[pltpu.VMEM((2 * size_rows, count_k), f32)],
-            compiler_params=pltpu.CompilerParams(vmem_limit_bytes=40 * 2**20),
-            name=f"middle{k}",
-        )(*operands)
+            [plane] * size_gy,
+            (where, green, tables, *gathered),
+            scratch=[
+                pltpu.VMEM((2 * size_rows, count_k), f32),
+                pltpu.VMEM((grid_x, green_sub, count_k), f32),
+                pltpu.VMEM((1, green_sub, count_k), f32),
+                pltpu.SemaphoreType.DMA((2,)),
+            ],
+            specs=[smem, hbm, vmem] + [vmem] * size_gy,
+        )
 
     last = []
     own = [exchange(v) for v in spectra]
@@ -306,6 +338,7 @@
     inv_im[:, 0] = sign_y
     inv_y = np.concatenate([inv_re, inv_im], 1) / long_y
     inv_y = split_table(inv_y.reshape(size_gy, brick_y, 2 * units))
+    inv_y = [jnp.asarray(v) for v in inv_y]
 
     def back_body(where_ref, high_ref, low_ref, *refs):
         ins, outs = refs[:CHUNKS], refs[CHUNKS:]

time: 150 us -> 135 us (0.900)
  local copies, waits for them, and re-layouts: 16.7 us -> 8.34 us
  Pallas kernels: 21.9 us -> 18.2 us
    pallas_call x2 -> x0, Pallas kernels: 11.5 us -> none  [middle(): pl.pallas_call(functools.partial(middle_body, k), grid=(1,), out_shape=[p...]
    unnamed x50 -> x20, local copies, waits for them, and re-layouts: 16.7 us -> 8.34 us
    pallas_call x4 -> x6, Pallas kernels: 10.4 us -> 18.2 us  [call(): pl.pallas_call(body, out_shape=out_shape, in_specs=specs or [vmem] * len(...]
  transfers between devices with their start and end apart: 8 -> 8, of which waited for: 6 -> 6; matrix products, arithmetic and copies ran while one was open for 1% -> 1% of each run, Pallas kernels for 8% -> 9%
where the time goes in v2:
time: 135 us
  waiting for transfers between devices  47.9 us (35%)
  blocking collectives  41.3 us (31%)
  Pallas kernels  18.2 us (13%)
  starting transfers between devices  17 us (13%)
  local copies, waits for them, and re-layouts  8.34 us (6%)
  other arithmetic  2.05 us (2%)
    ppermute x6, waiting for transfers between devices, shift(): return lax.ppermute(value, 'gy', perm)  47.9 us
    all_to_all x2, blocking collectives, exchange(): return lax.all_to_all(value, ('gx', 'gz'), 0, 0, tiled=True)  41.3 us
    pallas_call x6, Pallas kernels, call(): pl.pallas_call(body, out_shape=out_shape, in_specs=specs or [vmem] * len(...  18.2 us
    ppermute x6, starting transfers between devices, shift(): return lax.ppermute(value, 'gy', perm)  9.65 us
    unnamed x20, local copies, waits for them, and re-layouts  8.34 us
    all_to_all x2, starting transfers between devices, exchange(): return lax.all_to_all(value, ('gx', 'gz'), 0, 0, tiled=True)  7.31 us
  transfers between devices with their start and end apart: 8, of which 6 were waited for; matrix products, arithmetic and copies ran while one was open for 1% of the time, Pallas kernels for 9%

profile of v2, /device:TPU:0, one launch (start us, length us, event | category | flops | bytes accessed | tf_op | source)
XLA Modules:
  0.0 134.8 jit_solution(11052772422263504577)
XLA Ops:
  0.0 0.0 copy-start.2
  0.0 0.1 pad_add_fusion.where_ref
  0.1 0.0 copy-start.3
  0.1 1.4 %copy-done.3 = f32[64,64,32]{1,2,0:T(8,128)S(1)} copy-done((f32[64,64,32]{1,2,0:T(8,128)S(1)}, f32[64,64,32]{1,2,0:T(8,128)}, u32[]{:S(2)}) %copy-start.3) | copy-done | bytes 524312
  1.4 0.9 shard_map.73
  2.3 3.0 %collective-permute-start = (f32[64,1024]{1,0:T(8,128)S(1)}, f32[64,1024]{1,0:T(8,128)S(1)}, u32[]{:S(2)}, u32[]{:S(2)}) collective-permute-start(f32[64,1024]{1,0:T(8,128)S(1)} %get-tuple-element.16), channel_id=1, source_target_pairs={{0,4},{4,0},{1,5},{5,1},{2,6},{6,2},{3,7},{7,3},{8,12},{12,8},{9,1... | collective-permute-start | bytes 786440 | tf_op jit(solution)/shard_map/ppermute | solution.py:102
  5.3 6.3 %collective-permute-done.refs_1_ = f32[64,1024]{1,0:T(8,128)S(1)} collective-permute-done((f32[64,1024]{1,0:T(8,128)S(1)}, f32[64,1024]{1,0:T(8,128)S(1)}, u32[]{:S(2)}, u32[]{:S(2)}) %collective-permute-start) | collective-permute-done | bytes 262176 | tf_op jit(solution)/shard_map/ppermute | solution.py:102
  11.6 0.0 copy-start.6
  11.6 0.9 copy-done.6
  12.6 0.0 copy-start.7
  12.6 0.9 copy-done.7
  13.5 1.5 %shard_map.74 = (f32[16,64,128]{2,1,0:T(8,128)S(1)}, f32[16,64,128]{2,1,0:T(8,128)S(1)}) custom-call(s32[2]{0:T(128)S(1)} %pad_add_fusion.where_ref, bf16[2,256,64]{2,1,0:T(8,128)(2,1)S(1)} %copy-done.7, bf16[2,256,64]{2,1,0:T(8,128)(2,1)S(1)} %copy-done.6, f32[64,1024]{1,0:T(8,128)S(1)} %get-tuple-element.15.refs_0_, ...), custom_call_target="tpu_custom_call" | custom-call | tf_op jit(solution)/shard_map/pallas_call | solution.py:49
  14.9 0.0 copy-start.5
  15.0 21.6 %all_to_all.20.refs_0_ = f32[16,64,128]{2,1,0:T(8,128)S(1)} all-to-all(f32[16,64,128]{2,1,0:T(8,128)S(1)} %get-tuple-element.20), channel_id=1, replica_groups=mesh['gx'=4,'gy'=2,'gz'=4] {'gx','gz'}, dimensions={0} | all-to-all | bytes 1048576 | tf_op jit(solution)/shard_map/all_to_all | solution.py:148
  36.5 1.5 %collective-permute-start.3 = (f32[16,64,128]{2,1,0:T(8,128)S(1)}, f32[16,64,128]{2,1,0:T(8,128)}, u32[]{:S(2)}, u32[]{:S(2)}) collective-permute-start(f32[16,64,128]{2,1,0:T(8,128)S(1)} %all_to_all.20.refs_0_), channel_id=1, source_target_pairs={{0,4},{4,0},{1,5},{5,1},{2,6},{6,2},{3,7},{7,3},{8,12},{12,8},{9,1... | collective-permute-start | bytes 1572872 | tf_op jit(solution)/shard_map/ppermute | solution.py:102
  38.0 0.0 copy-done.5
  38.0 3.6 %all-to-all-start = ((f32[16,64,128]{2,1,0:T(8,128)}), f32[16,64,128]{2,1,0:T(8,128)S(1)}, u32[]{:S(2)}, u32[]{:S(2)}) async-start(f32[16,64,128]{2,1,0:T(8,128)} %copy-done.5), calls=%async_computation | async-start | bytes 1048576 | tf_op jit(solution)/shard_map/all_to_all | solution.py:148
  41.6 8.6 %collective-permute-done.3.refs_1_ = f32[16,64,128]{2,1,0:T(8,128)} collective-permute-done((f32[16,64,128]{2,1,0:T(8,128)S(1)}, f32[16,64,128]{2,1,0:T(8,128)}, u32[]{:S(2)}, u32[]{:S(2)}) %collective-permute-start.3) | collective-permute-done | bytes 524320 | tf_op jit(solution)/shard_map/ppermute | solution.py:102
  50.2 0.0 copy-done.2
  50.2 0.0 copy-start
  50.2 2.2 %copy-done = f32[512,16,128]{2,1,0:T(8,128)S(1)} copy-done((f32[512,16,128]{2,1,0:T(8,128)S(1)}, f32[512,16,128]{2,1,0:T(8,128)}, u32[]{:S(2)}) %copy-start) | copy-done | bytes 4194328
  52.4 6.1 %shard_map.76 = (f32[16,64,128]{2,1,0:T(8,128)S(1)}, f32[16,64,128]{2,1,0:T(8,128)}) custom-call(s32[2]{0:T(128)S(1)} %pad_add_fusion.where_ref, f32[512,16,128]{2,1,0:T(8,128)S(1)} %copy-done, bf16[4096,256]{1,0:T(8,128)(2,1)S(1)} %copy-done.2, f32[16,64,128]{2,1,0:T(8,128)S(1)} %all_to_all.20.refs_0_, f32[16,64,128]{2,1,0:T(8,128)} %collective-permute-done.3.refs_1_), custom_call_target="tpu_custom_call" | custom-call | tf_op jit(solution)/shard_map/pallas_call | solution.py:49
  58.5 0.0 copy-start.4
  58.5 0.8 copy-done.4
  59.3 1.5 %collective-permute-start.4 = (f32[16,64,128]{2,1,0:T(8,128)}, f32[16,64,128]{2,1,0:T(8,128)S(1)}, u32[]{:S(2)}, u32[]{:S(2)}) collective-permute-start(f32[16,64,128]{2,1,0:T(8,128)} %get-tuple-element.22), channel_id=1, source_target_pairs={{0,4},{4,0},{1,5},{5,1},{2,6},{6,2},{3,7},{7,3},{8,12},{12,8},{9,1... | collective-permute-start | bytes 1572872 | tf_op jit(solution)/shard_map/ppermute | solution.py:102
  60.8 0.0 all-to-all-done.refs_0_
  60.8 0.5 collective-permute-start.1
  61.4 13.0 %collective-permute-done.4 = f32[16,64,128]{2,1,0:T(8,128)S(1)} collective-permute-done((f32[16,64,128]{2,1,0:T(8,128)}, f32[16,64,128]{2,1,0:T(8,128)S(1)}, u32[]{:S(2)}, u32[]{:S(2)}) %collective-permute-start.4) | collective-permute-done | bytes 524320 | tf_op jit(solution)/shard_map/ppermute | solution.py:102
  74.3 1.9 %add.11 = f32[16,64,128]{2,1,0:T(8,128)} add(f32[16,64,128]{2,1,0:T(8,128)} %copy-done.4, f32[16,64,128]{2,1,0:T(8,128)S(1)} %collective-permute-done.4) | non-fusion elementwise | flops 131072 | bytes 1572864 | tf_op jit(solution)/shard_map/add | solution.py:331
  76.2 3.7 %all-to-all-start.3 = ((f32[16,64,128]{2,1,0:T(8,128)}), f32[16,64,128]{2,1,0:T(8,128)S(1)}, u32[]{:S(2)}, u32[]{:S(2)}) async-start(f32[16,64,128]{2,1,0:T(8,128)} %add.11), calls=%async_computation.3 | async-start | bytes 1048576 | tf_op jit(solution)/shard_map/all_to_all | solution.py:148
  80.0 3.6 %collective-permute-done.1.refs_1_ = f32[16,64,128]{2,1,0:T(8,128)} collective-permute-done((f32[16,64,128]{2,1,0:T(8,128)S(1)}, f32[16,64,128]{2,1,0:T(8,128)}, u32[]{:S(2)}, u32[]{:S(2)}) %collective-permute-start.1) | collective-permute-done | bytes 524320 | tf_op jit(solution)/shard_map/ppermute | solution.py:102
  83.6 0.0 copy-start.1
  83.6 2.2 %copy-done.1 = f32[512,16,128]{2,1,0:T(8,128)S(1)} copy-done((f32[512,16,128]{2,1,0:T(8,128)S(1)}, f32[512,16,128]{2,1,0:T(8,128)}, u32[]{:S(2)}) %copy-start.1) | copy-done | bytes 4194328
  85.8 0.0 copy-start.8
  85.8 0.0 copy-start.9
  85.8 6.6 %shard_map.75 = (f32[16,64,128]{2,1,0:T(8,128)S(1)}, f32[16,64,128]{2,1,0:T(8,128)S(1)}) custom-call(s32[2]{0:T(128)S(1)} %pad_add_fusion.where_ref, f32[512,16,128]{2,1,0:T(8,128)S(1)} %copy-done.1, bf16[4096,256]{1,0:T(8,128)(2,1)S(1)} %copy-done.2, f32[16,64,128]{2,1,0:T(8,128)S(1)} %all-to-all-done.refs_0_, f32[16,64,128]{2,1,0:T(8,128)} %collective-permute-done.1.refs_1_), custom_call_target="tpu_custom_call" | custom-call | tf_op jit(solution)/shard_map/pallas_call | solution.py:49
  92.4 1.5 %collective-permute-start.2 = (f32[16,64,128]{2,1,0:T(8,128)S(1)}, f32[16,64,128]{2,1,0:T(8,128)S(1)}, u32[]{:S(2)}, u32[]{:S(2)}) collective-permute-start(f32[16,64,128]{2,1,0:T(8,128)S(1)} %get-tuple-element.19), channel_id=1, source_target_pairs={{0,4},{4,0},{1,5},{5,1},{2,6},{6,2},{3,7},{7,3},{8,12},{12,8},{9,1... | collective-permute-start | bytes 1572872 | tf_op jit(solution)/shard_map/ppermute | solution.py:102
  93.9 9.8 %collective-permute-done.2 = f32[16,64,128]{2,1,0:T(8,128)S(1)} collective-permute-done((f32[16,64,128]{2,1,0:T(8,128)S(1)}, f32[16,64,128]{2,1,0:T(8,128)S(1)}, u32[]{:S(2)}, u32[]{:S(2)}) %collective-permute-start.2) | collective-permute-done | bytes 524320 | tf_op jit(solution)/shard_map/ppermute | solution.py:102
  103.8 0.1 add.10
  103.8 0.0 all-to-all-done.3.refs_1_
  103.8 19.8 %all_to_all.21.refs_0_ = f32[16,64,128]{2,1,0:T(8,128)S(1)} all-to-all(f32[16,64,128]{2,1,0:T(8,128)S(1)} %add.10), channel_id=1, replica_groups=mesh['gx'=4,'gy'=2,'gz'=4] {'gx','gz'}, dimensions={0} | all-to-all | bytes 1048576 | tf_op jit(solution)/shard_map/all_to_all | solution.py:148
  123.6 0.0 copy-done.8
  123.6 0.0 copy-done.9
  123.6 1.3 shard_map.77
  124.9 1.6 %collective-permute-start.5 = (f32[64,1024]{1,0:T(8,128)S(1)}, f32[64,1024]{1,0:T(8,128)S(1)}, u32[]{:S(2)}, u32[]{:S(2)}) collective-permute-start(f32[64,1024]{1,0:T(8,128)S(1)} %get-tuple-element.24), channel_id=1, source_target_pairs={{0,4},{4,0},{1,5},{5,1},{2,6},{6,2},{3,7},{7,3},{8,12},{12,8},{9,1... | collective-permute-start | bytes 786440 | tf_op jit(solution)/shard_map/ppermute | solution.py:102
  126.5 6.5 %collective-permute-done.5.refs_1_ = f32[64,1024]{1,0:T(8,128)S(1)} collective-permute-done((f32[64,1024]{1,0:T(8,128)S(1)}, f32[64,1024]{1,0:T(8,128)S(1)}, u32[]{:S(2)}, u32[]{:S(2)}) %collective-permute-start.5) | collective-permute-done | bytes 262176 | tf_op jit(solution)/shard_map/ppermute | solution.py:102
  133.0 1.9 %shard_map.78 = f32[64,32,64]{2,1,0:T(8,128)} custom-call(s32[2]{0:T(128)S(1)} %pad_add_fusion.where_ref, f32[64,1024]{1,0:T(8,128)S(1)} %get-tuple-element.23.refs_0_, f32[64,1024]{1,0:T(8,128)S(1)} %collective-permute-done.5.refs_1_), custom_call_target="tpu_custom_call" | custom-call | tf_op jit(solution)/shard_map/pallas_call | solution.py:49
Async XLA Ops:
  0.0 50.2 %copy-start.2 = (bf16[4096,256]{1,0:T(8,128)(2,1)S(1)}, bf16[4096,256]{1,0:T(8,128)(2,1)}, u32[]{:S(2)}) copy-start(bf16[4096,256]{1,0:T(8,128)(2,1)} %constant.28.clone.table_ref) | copy-start | bytes 6291460
  0.1 1.4 %copy-start.3 = (f32[64,64,32]{1,2,0:T(8,128)S(1)}, f32[64,64,32]{1,2,0:T(8,128)}, u32[]{:S(2)}) copy-start(f32[64,64,32]{1,2,0:T(8,128)} %param.7) | copy-start | bytes 1572868
  2.3 9.3 %collective-permute-start = (f32[64,1024]{1,0:T(8,128)S(1)}, f32[64,1024]{1,0:T(8,128)S(1)}, u32[]{:S(2)}, u32[]{:S(2)}) collective-permute-start(f32[64,1024]{1,0:T(8,128)S(1)} %get-tuple-element.16), channel_id=1, source_target_pairs={{0,4},{4,0},{1,5},{5,1},{2,6},{6,2},{3,7},{7,3},{8,12},{12,8},{9,1... | collective-permute-start | bytes 786440 | tf_op jit(solution)/shard_map/ppermute | solution.py:102
  11.6 0.9 copy-start.6
  12.6 0.9 copy-start.7
  14.9 23.1 %copy-start.5 = (f32[16,64,128]{2,1,0:T(8,128)}, f32[16,64,128]{2,1,0:T(8,128)S(1)}, u32[]{:S(2)}) copy-start(f32[16,64,128]{2,1,0:T(8,128)S(1)} %get-tuple-element.17) | copy-start | bytes 1572868
  36.5 13.7 %collective-permute-start.3 = (f32[16,64,128]{2,1,0:T(8,128)S(1)}, f32[16,64,128]{2,1,0:T(8,128)}, u32[]{:S(2)}, u32[]{:S(2)}) collective-permute-start(f32[16,64,128]{2,1,0:T(8,128)S(1)} %all_to_all.20.refs_0_), channel_id=1, source_target_pairs={{0,4},{4,0},{1,5},{5,1},{2,6},{6,2},{3,7},{7,3},{8,12},{12,8},{9,1... | collective-permute-start | bytes 1572872 | tf_op jit(solution)/shard_map/ppermute | solution.py:102
  38.0 22.8 %all-to-all-start = ((f32[16,64,128]{2,1,0:T(8,128)}), f32[16,64,128]{2,1,0:T(8,128)S(1)}, u32[]{:S(2)}, u32[]{:S(2)}) async-start(f32[16,64,128]{2,1,0:T(8,128)} %copy-done.5), calls=%async_computation | async-start | bytes 1048576 | tf_op jit(solution)/shard_map/all_to_all | solution.py:148
  50.2 2.2 %copy-start = (f32[512,16,128]{2,1,0:T(8,128)S(1)}, f32[512,16,128]{2,1,0:T(8,128)}, u32[]{:S(2)}) copy-start(f32[512,16,128]{2,1,0:T(8,128)} %green_hbm.3) | copy-start | bytes 12582916
  58.5 0.8 copy-start.4
  59.3 15.0 %collective-permute-start.4 = (f32[16,64,128]{2,1,0:T(8,128)}, f32[16,64,128]{2,1,0:T(8,128)S(1)}, u32[]{:S(2)}, u32[]{:S(2)}) collective-permute-start(f32[16,64,128]{2,1,0:T(8,128)} %get-tuple-element.22), channel_id=1, source_target_pairs={{0,4},{4,0},{1,5},{5,1},{2,6},{6,2},{3,7},{7,3},{8,12},{12,8},{9,1... | collective-permute-start | bytes 1572872 | tf_op jit(solution)/shard_map/ppermute | solution.py:102
  60.8 22.8 %collective-permute-start.1 = (f32[16,64,128]{2,1,0:T(8,128)S(1)}, f32[16,64,128]{2,1,0:T(8,128)}, u32[]{:S(2)}, u32[]{:S(2)}) collective-permute-start(f32[16,64,128]{2,1,0:T(8,128)S(1)} %all-to-all-done.refs_0_), channel_id=1, source_target_pairs={{0,4},{4,0},{1,5},{5,1},{2,6},{6,2},{3,7},{7,3},{8,12},{12,8},{9,1... | collective-permute-start | bytes 1572872 | tf_op jit(solution)/shard_map/ppermute | solution.py:102
  76.2 27.6 %all-to-all-start.3 = ((f32[16,64,128]{2,1,0:T(8,128)}), f32[16,64,128]{2,1,0:T(8,128)S(1)}, u32[]{:S(2)}, u32[]{:S(2)}) async-start(f32[16,64,128]{2,1,0:T(8,128)} %add.11), calls=%async_computation.3 | async-start | bytes 1048576 | tf_op jit(solution)/shard_map/all_to_all | solution.py:148
  83.6 2.2 %copy-start.1 = (f32[512,16,128]{2,1,0:T(8,128)S(1)}, f32[512,16,128]{2,1,0:T(8,128)}, u32[]{:S(2)}) copy-start(f32[512,16,128]{2,1,0:T(8,128)} %green_hbm.3) | copy-start | bytes 12582916
  85.8 37.8 %copy-start.8 = (bf16[2,64,256]{2,1,0:T(8,128)(2,1)S(1)}, bf16[2,64,256]{2,1,0:T(8,128)(2,1)}, u32[]{:S(2)}) copy-start(bf16[2,64,256]{2,1,0:T(8,128)(2,1)} %constant.30.clone.low_ref) | copy-start | bytes 196612
  85.8 37.8 %copy-start.9 = (bf16[2,64,256]{2,1,0:T(8,128)(2,1)S(1)}, bf16[2,64,256]{2,1,0:T(8,128)(2,1)}, u32[]{:S(2)}) copy-start(bf16[2,64,256]{2,1,0:T(8,128)(2,1)} %constant.29.clone.high_ref) | copy-start | bytes 196612
  92.4 11.4 %collective-permute-start.2 = (f32[16,64,128]{2,1,0:T(8,128)S(1)}, f32[16,64,128]{2,1,0:T(8,128)S(1)}, u32[]{:S(2)}, u32[]{:S(2)}) collective-permute-start(f32[16,64,128]{2,1,0:T(8,128)S(1)} %get-tuple-element.19), channel_id=1, source_target_pairs={{0,4},{4,0},{1,5},{5,1},{2,6},{6,2},{3,7},{7,3},{8,12},{12,8},{9,1... | collective-permute-start | bytes 1572872 | tf_op jit(solution)/shard_map/ppermute | solution.py:102
  124.9 8.1 %collective-permute-start.5 = (f32[64,1024]{1,0:T(8,128)S(1)}, f32[64,1024]{1,0:T(8,128)S(1)}, u32[]{:S(2)}, u32[]{:S(2)}) collective-permute-start(f32[64,1024]{1,0:T(8,128)S(1)} %get-tuple-element.24), channel_id=1, source_target_pairs={{0,4},{4,0},{1,5},{5,1},{2,6},{6,2},{3,7},{7,3},{8,12},{12,8},{9,1... | collective-permute-start | bytes 786440 | tf_op jit(solution)/shard_map/ppermute | solution.py:102
